TPU v7x, 32 devices: a whole 2x2x4 slice. The times are simulated.
32 devices in a mesh: mem: 4 (over x, core), tile: 8 (over z, y).
Axes of the slice: x: 2, y: 2, z: 4, core: 2. Of those that a mesh axis runs over, the one named last changes fastest.
Arguments:
- alpha: bfloat16 [80, 64, 32, 128], P('mem', 'tile'), may hold values from -0.8984375 to 0.8984375
- ensemble: bfloat16 [80, 3, 64, 32, 128], P('mem', None, 'tile'), may hold values from -6 to 6
- loc_vert: bfloat16 [128, 128], replicated, may hold values from -0.25 to 1.5, as said below
- obs_col: int32 [8, 2048], P('tile'), may hold values from 0 to 1023
- obs_lev: int32 [8, 2048], P('tile'), may hold values from 0 to 127
- obs_count: int32 [8], P('tile'), may hold values from 512 to 2048
- innovation: float32 [8, 2048], P('tile'), may hold values from -6 to 6
- obs_weight: float32 [8, 2048], P('tile'), may hold values from 1 to 8
Outputs:
- gradient: float32 [80, 64, 32, 128], P('mem', 'tile')
Inputs may be any that keep to these rules, and one draw needn't show every extreme that they name: `loc_vert`: a square root of the vertical localization, applied along levels.
All inputs are finite; a program needn't handle non-finite values.
Results may differ from a plain program's by a relative error of at most 0.0019.
Values sent between devices are 32-bit elements; how exact they have to be, the bound alone decides.
A program may use at most 64 MiB of HBM per device.

v0:
```python
import functools

import jax
import jax.numpy as jnp
from jax import lax
from jax.experimental import pallas as pl
from jax.experimental.pallas import tpu as pltpu
from jax.sharding import PartitionSpec as P

V = 3
F32 = jnp.float32
BF16 = jnp.bfloat16
MESH = pl.DeviceIdType.MESH


def split2(x):
    hi = x.astype(BF16)
    lo = (x - hi.astype(F32)).astype(BF16)
    return hi, lo


def dot(a, b):
    return jnp.dot(a, b, preferred_element_type=F32)


def dot_nt(a, b):
    return lax.dot_general(a, b, (((1,), (1,)), ((), ())), preferred_element_type=F32)


def band(distance):
    d = jnp.abs(distance)
    return jnp.where(d == 0, 6.0, jnp.where(d == 1, 4.0, jnp.where(d == 2, 1.0, 0.0)))


def column_weight(c, c2, cols):
    end = (c == c2) & ((c == 0) | (c == cols - 1))
    return (band(c - c2) - jnp.where(end, 1.0, 0.0)) * (1.0 / 16.0)


def kernel(n, tiles, chunks, alpha, ens_hbm, loc, col, lev, cnt, innov, wgt, out,
           ens, hs, hr, gs, gr, lbe, mm, em, wt, inci, ince, reci, rece, redi, rede,
           incf, incg, ihalo, adj, adjs, ahalo,
           ens_sem, hs_sem, hr_sem, gs_sem, gr_sem, rs_s, rs_r, ag_s, ag_r, ih_s, ih_r, ah_s, ah_r):
    members, rows, cols, levels = alpha.shape
    size = rows * cols
    cq = cols // n
    per = members // chunks
    m = lax.axis_index("mem")
    t = lax.axis_index("tile")
    has = (t > 0, t < tiles - 1)
    near = (t - 1, t + 1)
    ens_copy = pltpu.make_async_copy(ens_hbm, ens, ens_sem)
    ens_copy.start()

    barrier = pltpu.get_barrier_semaphore()
    for d in range(1, n):
        pl.semaphore_signal(barrier, inc=1, device_id={"mem": lax.rem(m + d, n), "tile": t}, device_id_type=MESH)
    for s in range(2):
        @pl.when(has[s])
        def _(s=s):
            for d in range(n):
                pl.semaphore_signal(barrier, inc=1, device_id={"mem": lax.rem(m + d, n), "tile": near[s]}, device_id_type=MESH)

    hs[0] = alpha[:, 0:2].astype(F32)
    hs[1] = alpha[:, rows - 2 : rows].astype(F32)
    pl.semaphore_wait(barrier, n - 1 + n * (has[0].astype(jnp.int32) + has[1].astype(jnp.int32)))

    def halo(src, dst, ssem, rsem, s):
        return pltpu.make_async_remote_copy(
            src_ref=src, dst_ref=dst, send_sem=ssem, recv_sem=rsem,
            device_id={"mem": m, "tile": near[s]}, device_id_type=MESH)

    def edge_copy(src, dst, ssem, rsem, s, c):
        part = pl.ds(c * per, per)
        return halo(src.at[s, part], dst.at[1 - s, part], ssem.at[s, c], rsem.at[1 - s, c], s)

    for c in range(chunks):
        for s in range(2):
            @pl.when(has[s])
            def _(s=s, c=c):
                edge_copy(hs, hr, hs_sem, hr_sem, s, c).start()
    for s in range(2):
        @pl.when(jnp.logical_not(has[s]))
        def _(s=s):
            hr[s] = jnp.zeros(hr.shape[1:], F32)
            gr[s] = jnp.zeros(gr.shape[1:], F32)
            ihalo[s] = jnp.zeros(ihalo.shape[1:], F32)
            ahalo[s] = jnp.zeros(ahalo.shape[1:], F32)

    i = lax.broadcasted_iota(jnp.int32, (size, size), 0)
    j = lax.broadcasted_iota(jnp.int32, (size, size), 1)
    r, r2 = lax.div(i, cols), lax.div(j, cols)
    end = (r == r2) & (((r == 0) & (t == 0)) | ((r == rows - 1) & (t == tiles - 1)))
    row_weight = (band(r - r2) - jnp.where(end, 1.0, 0.0)) * (1.0 / 16.0)
    mm[...] = (row_weight * column_weight(i - r * cols, j - r2 * cols, cols)).astype(BF16)
    i = lax.broadcasted_iota(jnp.int32, (4 * cols, 4 * cols), 0)
    j = lax.broadcasted_iota(jnp.int32, (4 * cols, 4 * cols), 1)
    q, q2 = lax.div(i, cols), lax.div(j, cols)
    r = jnp.where(q < 2, q, q + rows - 4)
    r2 = jnp.where(q2 < 2, q2 - 2, q2 - 2 + rows)
    em[...] = (band(r - r2) * (1.0 / 16.0) * column_weight(i - q * cols, j - q2 * cols, cols)).astype(BF16)

    inci[...] = jnp.zeros_like(inci)
    ince[...] = jnp.zeros_like(ince)
    ens_copy.wait()
    lv = loc[...]

    def lift(k, carry):
        hi, lo = split2(dot(mm[...], alpha[k].reshape(size, levels)))
        base = (dot_nt(hi, lv) + dot_nt(lo, lv)).reshape(rows, cols, levels)
        lbe[k, 0:2] = base[0:2]
        lbe[k, 2:4] = base[rows - 2 : rows]
        inner = base[2 : rows - 2].astype(BF16).astype(F32)
        for v in range(V):
            inci[v] += ens[k, v, 2 : rows - 2].astype(F32) * inner
        return carry

    lax.fori_loop(0, members, lift, 0)

    def spread_copy(part, rec, d, which):
        peer = lax.rem(m + d, n)
        return pltpu.make_async_remote_copy(
            src_ref=part.at[:, :, pl.ds(pl.multiple_of(peer * cq, cq), cq), :], dst_ref=rec.at[d - 1],
            send_sem=rs_s.at[which, d - 1], recv_sem=rs_r.at[which, d - 1],
            device_id={"mem": peer, "tile": t}, device_id_type=MESH)

    def gather_copy(red, full, d, which):
        peer = lax.rem(m + d, n)
        return pltpu.make_async_remote_copy(
            src_ref=red, dst_ref=full.at[:, :, pl.ds(pl.multiple_of(m * cq, cq), cq), :],
            send_sem=ag_s.at[which, d - 1], recv_sem=ag_r.at[which, d - 1],
            device_id={"mem": peer, "tile": t}, device_id_type=MESH)

    def ihalo_copy(s, slot, d):
        return pltpu.make_async_remote_copy(
            src_ref=rede.at[:, 3 * s], dst_ref=ihalo.at[slot, :, pl.ds(pl.multiple_of(m * cq, cq), cq), :],
            send_sem=ih_s.at[s, d], recv_sem=ih_r.at[slot, d],
            device_id={"mem": lax.rem(m + d, n), "tile": near[s]}, device_id_type=MESH)

    def reduce(part, rec, red, full, which):
        mine = pl.ds(pl.multiple_of(m * cq, cq), cq)
        for d in range(1, n):
            spread_copy(part, rec, d, which).start()
        total = part[:, :, mine, :]
        for d in range(1, n):
            spread_copy(part, rec, d, which).wait_recv()
            total = total + rec[d - 1]
        red[...] = total
        if which == 1:
            for s in range(2):
                @pl.when(has[s])
                def _(s=s):
                    for d in range(n):
                        ihalo_copy(s, 1 - s, d).start()
        for d in range(1, n):
            gather_copy(red, full, d, which).start()
        full[:, :, mine, :] = total

    def finish(part, rec, red, full, which):
        for d in range(1, n):
            gather_copy(red, full, d, which).wait_recv()
        for d in range(1, n):
            spread_copy(part, rec, d, which).wait_send()
            gather_copy(red, full, d, which).wait_send()

    reduce(inci, reci, redi, incf, 0)

    slots = col.shape[1]
    place = col[...]
    wide = 2 * cols
    frow = lax.div(place, wide)
    fcol = place - frow * wide
    slot = lax.broadcasted_iota(jnp.int32, (1, slots), 1)
    variable = lax.rem(slot, V)

    def weights(fine, count, shift):
        main = lax.div(fine, 2)
        other = jnp.where(fine - 2 * main == 1, main + 1, main - 1)
        at = lax.broadcasted_iota(jnp.int32, (count, slots), 0) - shift
        return jnp.where(at == main, 0.75, 0.0) + jnp.where(at == other, 0.25, 0.0)

    wr = weights(frow, rows + 2, 1)
    wc = weights(fcol, cols, 0)
    for v in range(V):
        mask = jnp.where(variable == v, 1.0, 0.0)
        for a in range(rows + 2):
            start = (a * V + v) * cols
            wt[start : start + cols, :] = (wc * (wr[a : a + 1, :] * mask)).astype(BF16)
    finish(inci, reci, redi, incf, 0)

    for c in range(chunks):
        for s in range(2):
            @pl.when(has[s])
            def _(s=s, c=c):
                part = pl.ds(c * per, per)
                halo(hs.at[s, part], hr.at[s, part], hs_sem.at[s, c], hr_sem.at[s, c], s).wait_recv()

        def lift_edge(k, carry):
            around = jnp.concatenate([hr[0, k], hr[1, k]], axis=0).astype(BF16).reshape(4 * cols, levels)
            hi, lo = split2(dot(em[...], around))
            edge = (dot_nt(hi, lv) + dot_nt(lo, lv)).reshape(4, cols, levels) + lbe[k]
            edge = edge.astype(BF16).astype(F32)
            for v in range(V):
                ince[v, 0:2] += ens[k, v, 0:2].astype(F32) * edge[0:2]
                ince[v, 2:4] += ens[k, v, rows - 2 : rows].astype(F32) * edge[2:4]
            return carry

        lax.fori_loop(c * per, (c + 1) * per, lift_edge, 0)

    reduce(ince, rece, rede, incg, 1)
    finish(ince, rece, rede, incg, 1)

    for s in range(2):
        @pl.when(has[s])
        def _(s=s):
            for d in range(n):
                ihalo_copy(s, s, d).wait_recv()
                ihalo_copy(s, 1 - s, d).wait_send()

    places = V * (rows + 2) * cols
    pieces = [ihalo[0], incg[:, 0], incg[:, 1]] + [incf[:, a] for a in range(rows - 4)]
    pieces += [incg[:, 2], incg[:, 3], ihalo[1]]
    whole = jnp.concatenate(pieces, axis=0).reshape(places, levels)
    flipped = whole.T
    hi, lo = split2(flipped)
    picked = dot(hi, wt[...]) + dot(lo, wt[...])
    hot = lax.broadcasted_iota(jnp.int32, (levels, slots), 0) == lev[...]
    value = jnp.sum(jnp.where(hot, picked, 0.0), axis=0, keepdims=True)
    weighted = jnp.where(slot < cnt[0], wgt[...] * (value - innov[...]), 0.0)
    sent = jnp.where(hot, jnp.broadcast_to(weighted, hot.shape), 0.0)
    hi, lo = split2(sent)
    sent2 = jnp.concatenate([hi, lo], axis=0)

    def adjoint(a, count):
        both = dot_nt(wt[a * V * cols : (a + count) * V * cols, :], sent2)
        return (both[:, :levels] + both[:, levels:]).reshape(count, V, cols, levels)

    adjs[0] = adjoint(0, 1)[0]
    adjs[1] = adjoint(rows + 1, 1)[0]

    def ahalo_copy(s, slot_there):
        return halo(adjs.at[s], ahalo.at[slot_there], ah_s.at[s], ah_r.at[slot_there], s)

    for s in range(2):
        @pl.when(has[s])
        def _(s=s):
            ahalo_copy(s, 1 - s).start()
    top, bottom = adjoint(1, 2), adjoint(rows - 1, 2)
    for a in range(2):
        adj[:, a] = top[a]
        adj[:, rows - 2 + a] = bottom[a]

    def field(k, low, high):
        total = ens[k, 0, low:high].astype(F32) * adj[0, low:high]
        for v in range(1, V):
            total = total + ens[k, v, low:high].astype(F32) * adj[v, low:high]
        return total

    def back_copy(s, slot, w, c):
        part = pl.ds(c * per, per)
        return halo(gs.at[s, w, part], gr.at[slot, w, part], gs_sem.at[s, w, c], gr_sem.at[slot, w, c], s)

    def send_row(w):
        where = (1 - w, rows - 2 + w)
        for c in range(chunks):
            def edges(k, carry):
                for s in range(2):
                    gs[s, w, k] = field(k, where[s], where[s] + 1)[0]
                return carry

            lax.fori_loop(c * per, (c + 1) * per, edges, 0)
            for s in range(2):
                @pl.when(has[s])
                def _(s=s, c=c):
                    back_copy(s, 1 - s, w, c).start()

    send_row(0)
    for s in range(2):
        @pl.when(has[s])
        def _(s=s):
            ahalo_copy(s, s).wait_recv()
            ahalo_copy(s, 1 - s).wait_send()
    adj[:, 0] += ahalo[0]
    adj[:, rows - 1] += ahalo[1]
    send_row(1)
    inner = adjoint(3, rows - 4)
    for a in range(rows - 4):
        adj[:, 2 + a] = inner[a]

    def raised(x):
        hi, lo = split2(x)
        return split2(dot(hi, lv) + dot(lo, lv))

    def inside(k, carry):
        middle = field(k, 2, rows - 2).reshape(size - 4 * cols, levels)
        g = jnp.concatenate([gs[0, 1, k], gs[0, 0, k], middle, gs[1, 0, k], gs[1, 1, k]], axis=0)
        hi, lo = raised(g)
        back = dot(mm[...], hi) + dot(mm[...], lo)
        out[k] = alpha[k].astype(F32) + back.reshape(rows, cols, levels)
        return carry

    lax.fori_loop(0, members, inside, 0)

    for c in range(chunks):
        for s in range(2):
            @pl.when(has[s])
            def _(s=s, c=c):
                for w in range(2):
                    back_copy(s, s, w, c).wait_recv()

        def outer(k, carry):
            around = jnp.concatenate([gr[0, 0, k], gr[0, 1, k], gr[1, 1, k], gr[1, 0, k]], axis=0)
            hi, lo = raised(around)
            back = (dot(em[...], hi) + dot(em[...], lo)).reshape(4, cols, levels)
            out[k, 0:2] += back[0:2]
            out[k, rows - 2 : rows] += back[2:4]
            return carry

        lax.fori_loop(c * per, (c + 1) * per, outer, 0)
    for c in range(chunks):
        for s in range(2):
            @pl.when(has[s])
            def _(s=s, c=c):
                edge_copy(hs, hr, hs_sem, hr_sem, s, c).wait_send()
                for w in range(2):
                    back_copy(s, 1 - s, w, c).wait_send()


def solution(mesh):
    n = mesh.shape["mem"]
    tiles = mesh.shape["tile"]

    def on_device(alpha, ensemble, loc_vert, obs_col, obs_lev, obs_count, innovation, obs_weight):
        members, rows, cols, levels = alpha.shape
        slots = obs_col.shape[1]
        chunks = 4 if members % 4 == 0 else 1
        cq = cols // n
        vmem = pl.BlockSpec(memory_space=pltpu.VMEM)
        edge = pltpu.VMEM((2, members, 2, cols, levels), F32)
        turned = pltpu.VMEM((2, 2, members, cols, levels), F32)
        dma = pltpu.SemaphoreType.DMA
        return pl.pallas_call(
            functools.partial(kernel, n, tiles, chunks),
            out_shape=jax.ShapeDtypeStruct(alpha.shape, F32),
            in_specs=[vmem, pl.BlockSpec(memory_space=pl.ANY), vmem, vmem, vmem,
                      pl.BlockSpec(memory_space=pltpu.SMEM), vmem, vmem],
            out_specs=vmem,
            scratch_shapes=[
                pltpu.VMEM(ensemble.shape, BF16), edge, edge, turned, turned,
                pltpu.VMEM((members, 4, cols, levels), F32),
                pltpu.VMEM((rows * cols, rows * cols), BF16),
                pltpu.VMEM((4 * cols, 4 * cols), BF16),
                pltpu.VMEM((V * (rows + 2) * cols, slots), BF16),
                pltpu.VMEM((V, rows - 4, cols, levels), F32),
                pltpu.VMEM((V, 4, cols, levels), F32),
                pltpu.VMEM((n - 1, V, rows - 4, cq, levels), F32),
                pltpu.VMEM((n - 1, V, 4, cq, levels), F32),
                pltpu.VMEM((V, rows - 4, cq, levels), F32),
                pltpu.VMEM((V, 4, cq, levels), F32),
                pltpu.VMEM((V, rows - 4, cols, levels), F32),
                pltpu.VMEM((V, 4, cols, levels), F32),
                pltpu.VMEM((2, V, cols, levels), F32),
                pltpu.VMEM((V, rows, cols, levels), F32),
                pltpu.VMEM((2, V, cols, levels), F32),
                pltpu.VMEM((2, V, cols, levels), F32),
                dma, dma((2, chunks)), dma((2, chunks)), dma((2, 2, chunks)), dma((2, 2, chunks)),
                dma((2, n - 1)), dma((2, n - 1)), dma((2, n - 1)), dma((2, n - 1)),
                dma((2, n)), dma((2, n)), dma((2,)), dma((2,)),
            ],
            compiler_params=pltpu.CompilerParams(
                collective_id=0, has_side_effects=True, vmem_limit_bytes=50 << 20),
        )(alpha, ensemble, loc_vert, obs_col, obs_lev, obs_count, innovation, obs_weight)

    in_specs = (
        P("mem", "tile", None, None),
        P("mem", None, "tile", None, None),
        P(),
        P("tile", None),
        P("tile", None),
        P("tile"),
        P("tile", None),
        P("tile", None),
    )
    out_specs = P("mem", "tile", None, None)
    return jax.shard_map(
        on_device, mesh=mesh, in_specs=in_specs, out_specs=out_specs, check_vma=False
    )
```

profile of v0, /device:TPU:16, one launch (start us, length us, event | category | flops | bytes accessed | tf_op | source)
XLA Modules:
  0.0 86.5 jit_solution(14663157178745655259)
XLA Ops:
  0.7 0.0 copy-start
  0.7 1.3 %copy-done = bf16[20,8,32,128]{3,2,1,0:T(8,128)(2,1)S(1)} copy-done((bf16[20,8,32,128]{3,2,1,0:T(8,128)(2,1)S(1)}, bf16[20,8,32,128]{3,2,1,0:T(8,128)(2,1)}, u32[]{:S(2)}) %copy-start) | copy-done | bytes 1310744
  2.0 0.0 copy-start.1
  2.0 0.8 copy-done.1
  2.7 0.0 copy-start.2
  2.7 0.7 copy-done.2
  3.4 0.0 copy-start.3
  3.4 0.7 copy-done.3
  4.1 0.0 copy-start.4
  4.1 0.7 copy-done.4
  4.8 0.0 copy-start.5
  4.8 0.7 copy-done.5
  5.5 79.5 %shard_map.82 = f32[20,8,32,128]{3,2,1,0:T(8,128)S(1)} custom-call(bf16[20,8,32,128]{3,2,1,0:T(8,128)(2,1)S(1)} %copy-done, bf16[20,3,8,32,128]{4,3,2,1,0:T(8,128)(2,1)} %ens_hbm.1, bf16[128,128]{1,0:T(8,128)(2,1)S(1)} %copy-done.1, s32[1,2048]{1,0:T(1,128)S(1)} %copy-done.2, s32[1,2048]{1,0:T(1,128)S(1)} %copy-done.3, s32[1]{0:T(128)S(6)} %copy.10.cnt, ...), custom_call_target="tpu_custom_call" | custom-call | tf_op jit(solution)/shard_map/pallas_call | solution.py:342
  85.0 1.5 %copy.11 = f32[20,8,32,128]{3,2,1,0:T(8,128)} copy(f32[20,8,32,128]{3,2,1,0:T(8,128)S(1)} %shard_map.82) | data formatting | bytes 5242880
Async XLA Ops:
  0.7 1.3 %copy-start = (bf16[20,8,32,128]{3,2,1,0:T(8,128)(2,1)S(1)}, bf16[20,8,32,128]{3,2,1,0:T(8,128)(2,1)}, u32[]{:S(2)}) copy-start(bf16[20,8,32,128]{3,2,1,0:T(8,128)(2,1)} %alpha.1) | copy-start | bytes 3932164
  2.0 0.8 copy-start.1
  2.7 0.7 copy-start.2
  3.4 0.7 copy-start.3
  4.1 0.7 copy-start.4
  4.8 0.7 copy-start.5
where the time goes:
time: 88.1 us; the launch traced here: 86.5 us
  Pallas kernels  79.5 us (90%)
  local copies, waits for them, and re-layouts  6.35 us (7%)
    pallas_call x1, Pallas kernels, on_device(): pl.pallas_call(functools.partial(kernel, n, tiles, chunks), out_shape=jax...  79.5 us
    unnamed x13, local copies, waits for them, and re-layouts  6.35 us

commit v1 on v0

v1 whole, which is shorter than its diff:
```python
import functools

import jax
import jax.numpy as jnp
from jax import lax
from jax.experimental import pallas as pl
from jax.experimental.pallas import tpu as pltpu
from jax.sharding import PartitionSpec as P

V = 3
F32 = jnp.float32
BF16 = jnp.bfloat16
MESH = pl.DeviceIdType.MESH


def split2(x):
    hi = x.astype(BF16)
    lo = (x - hi.astype(F32)).astype(BF16)
    return hi, lo


def dot(a, b):
    return jnp.dot(a, b, preferred_element_type=F32)


def dot_nt(a, b):
    return lax.dot_general(a, b, (((1,), (1,)), ((), ())), preferred_element_type=F32)


def band(distance):
    d = jnp.abs(distance)
    return jnp.where(d == 0, 6.0, jnp.where(d == 1, 4.0, jnp.where(d == 2, 1.0, 0.0)))


def column_weight(c, c2, cols):
    end = (c == c2) & ((c == 0) | (c == cols - 1))
    return (band(c - c2) - jnp.where(end, 1.0, 0.0)) * (1.0 / 16.0)


def kernel(n, tiles, chunks, alpha_h, ens_h, loc_h, col_h, lev_h, cnt, innov_h, wgt_h, out,
           av, ens, loc, col, lev, innov, wgt,
           hs, hr, hl, gs, gr, gl, mm, sc, em, wt, w15, sent, e15,
           bi, bi1, bi2, fi, b0, b01, b02, f0, b1, b11, b12, f1,
           ihalo, adj, adjs, ahalo, adjs15, ahalo15, gs15, gr15,
           in_sem, hs_s, hs_r, hl_s, hl_r, gs_s, gs_r, gl_s, gl_r,
           sh_s, sh_r, ih_s, ih_r, ah_s, ah_r, a15_s, a15_r, g15_s, g15_r):
    members, rows, cols, levels = out.shape
    size = rows * cols
    ch = cols // 2
    mid = (rows - 4) // 2
    per = members // chunks
    group = 4 if members % 4 == 0 else 1
    slots = col.shape[1]
    m = lax.axis_index("mem")
    t = lax.axis_index("tile")
    p = lax.rem(m, 2)
    mate = m + 1 - 2 * p
    has = (t > 0, t < tiles - 1)
    near = (t - 1, t + 1)
    edge = (slice(0, 2), slice(rows - 2, rows))
    half = (slice(0, ch), slice(ch, cols))

    def loads():
        pairs = (
            (alpha_h.at[:, 0:2], av.at[:, 0:2]),
            (alpha_h.at[:, rows - 2 : rows], av.at[:, rows - 2 : rows]),
            (loc_h, loc),
            (alpha_h.at[:, 2 : rows - 2], av.at[:, 2 : rows - 2]),
            (ens_h, ens),
            (col_h, col), (lev_h, lev), (innov_h, innov), (wgt_h, wgt))
        return [pltpu.make_async_copy(a, b, in_sem.at[i]) for i, (a, b) in enumerate(pairs)]

    copies = loads()
    for copy in copies:
        copy.start()

    relays = tiles % 2 == 0 and tiles >= 4
    odd = lax.rem(t, 2)
    turn = tiles // 2
    share_out = lax.div(chunks * lax.div(t + odd, 2), max(turn, 1))
    n_out = odd * (chunks - share_out) + (1 - odd) * share_out
    share_in = lax.div(chunks * lax.div(t + 2 - 3 * odd, 2), max(turn, 1))
    n_in = (1 - odd) * (chunks - share_in) + odd * share_in
    far = (t >= 2, t <= tiles - 3)
    passes = jnp.where(odd == 1, t - 2, tiles - 3 - t) >= 0

    barrier = pltpu.get_barrier_semaphore()

    def greet(who, where):
        pl.semaphore_signal(barrier, inc=1, device_id={"mem": who, "tile": where}, device_id_type=MESH)

    for d in range(1, n):
        greet(lax.rem(m + d, n), t)
    total = jnp.int32(n - 1)
    for s in range(2):
        @pl.when(has[s])
        def _(s=s):
            greet(m, near[s])
            greet(mate, near[s])
        total = total + 2 * has[s].astype(jnp.int32)
        if relays:
            @pl.when(far[s])
            def _(s=s):
                greet(m, t - 2 + 4 * s)
            total = total + far[s].astype(jnp.int32)

    def remote(src, dst, ssem, rsem, who, where):
        return pltpu.make_async_remote_copy(
            src_ref=src, dst_ref=dst, send_sem=ssem, recv_sem=rsem,
            device_id={"mem": who, "tile": where}, device_id_type=MESH)

    class Halo:
        def __init__(self, src, dst, via, ss, sr, vs, vr):
            self.src, self.dst, self.via = src, dst, via
            self.ss, self.sr, self.vs, self.vr = ss, sr, vs, vr

        def direct(self, h, s, c):
            part = pl.ds(c * per, per)
            return remote(self.src.at[h, s, part], self.dst.at[h, 1 - s, part],
                          self.ss.at[h, s, c], self.sr.at[h, 1 - s, c], m, near[s])

        def detour(self, h, s, c):
            part = pl.ds(c * per, per)
            return remote(self.src.at[h, s, part], self.via.at[h, part],
                          self.ss.at[h, s, c], self.vr.at[h, c], m, t + 1 - 2 * odd)

        def onward(self, h, c):
            part = pl.ds(c * per, per)
            return remote(self.via.at[h, part], self.dst.at[h, odd, part],
                          self.vs.at[h, c], self.sr.at[h, odd, c], m, t + 2 - 4 * odd)

        def send(self, h, c):
            for s in range(2):
                if relays:
                    turned = (odd == s) & (c >= chunks - n_out)

                    @pl.when(has[s] & turned)
                    def _(s=s):
                        self.detour(h, s, c).start()

                    @pl.when(has[s] & jnp.logical_not(turned))
                    def _(s=s):
                        self.direct(h, s, c).start()
                else:
                    @pl.when(has[s])
                    def _(s=s):
                        self.direct(h, s, c).start()

        def forward(self, h, c):
            if relays:
                @pl.when(passes & (c >= chunks - n_in))
                def _():
                    self.onward_recv(h, c).wait_recv()
                    self.onward(h, c).start()

        def onward_recv(self, h, c):
            part = pl.ds(c * per, per)
            return remote(self.via.at[h, part], self.via.at[h, part],
                          self.vs.at[h, c], self.vr.at[h, c], m, t + 1 - 2 * odd)

        def receive(self, h, c):
            for s in range(2):
                @pl.when(has[s])
                def _(s=s):
                    part = pl.ds(c * per, per)
                    remote(self.dst.at[h, s, part], self.dst.at[h, s, part],
                           self.ss.at[h, s, c], self.sr.at[h, s, c], m, near[s]).wait_recv()

        def drain(self):
            for h in range(2):
                for c in range(chunks):
                    for s in range(2):
                        @pl.when(has[s])
                        def _(h=h, s=s, c=c):
                            self.direct(h, s, c).wait_send()
                    if relays:
                        @pl.when(passes & (c >= chunks - n_in))
                        def _(h=h, c=c):
                            self.onward(h, c).wait_send()

    first = Halo(hs, hr, hl, hs_s, hs_r, hl_s, hl_r)
    second = Halo(gs, gr, gl, gs_s, gs_r, gl_s, gl_r)
    order = list(range(chunks - 1, -1, -1))

    i = lax.broadcasted_iota(jnp.int32, (4 * cols, 4 * cols), 0)
    j = lax.broadcasted_iota(jnp.int32, (4 * cols, 4 * cols), 1)
    q, q2 = lax.div(i, cols), lax.div(j, cols)
    across = column_weight(i - q * cols, j - q2 * cols, cols)
    sc[...] = (jnp.where(q == q2, 1.0 / 16.0, 0.0) * across).astype(BF16)
    r = jnp.where(q < 2, q, q + rows - 4)
    r2 = jnp.where(q2 < 2, q2 - 2, q2 - 2 + rows)
    corner = (band(r - r2) * (1.0 / 16.0) * across).astype(BF16)
    em[:, 0 : 4 * cols] = corner
    em[:, 4 * cols :] = corner

    for k in range(3):
        copies[k].wait()
    lv = loc[...]
    lv_nt = jnp.concatenate([lv, lv], axis=1)
    lv_nn = jnp.concatenate([lv, lv], axis=0)

    def prepare(k):
        x = jnp.concatenate([av[k, 0:2], av[k, rows - 2 : rows]], axis=0).reshape(4 * cols, levels)
        both = jnp.concatenate(split2(dot(sc[...], x)), axis=1)
        u = dot_nt(both, lv_nt).reshape(4, cols, levels)
        for s in range(2):
            for h in range(2):
                hs[h, s, k] = u[2 * s : 2 * s + 2, half[h]]

    entered = False
    for c in order:
        for k in range(c * per, (c + 1) * per):
            prepare(k)
        if not entered:
            pl.semaphore_wait(barrier, total)
            entered = True
        first.send(0, c)
    for c in order[: chunks // 2]:
        first.send(1, c)
    for s in range(2):
        @pl.when(jnp.logical_not(has[s]))
        def _(s=s):
            for ref in (hr, gr):
                for h in range(2):
                    ref[h, s] = jnp.zeros(ref.shape[2:], F32)
            for ref in (ihalo, ahalo):
                for h in range(2):
                    ref[h, s] = jnp.zeros(ref.shape[2:], F32)
            ahalo15[s] = jnp.zeros(ahalo15.shape[1:], F32)
            gr15[s] = jnp.zeros(gr15.shape[1:], F32)

    i = lax.broadcasted_iota(jnp.int32, (size, size), 0)
    j = lax.broadcasted_iota(jnp.int32, (size, size), 1)
    r, r2 = lax.div(i, cols), lax.div(j, cols)
    end = (r == r2) & (((r == 0) & (t == 0)) | ((r == rows - 1) & (t == tiles - 1)))
    row_weight = (band(r - r2) - jnp.where(end, 1.0, 0.0)) * (1.0 / 16.0)
    mm[...] = (row_weight * column_weight(i - r * cols, j - r2 * cols, cols)).astype(BF16)

    stage_refs = ((b0, b01, b02, f0), (b1, b11, b12, f1), (bi, bi1, bi2, fi))
    for ref in (b0, b1, bi):
        ref[...] = jnp.zeros_like(ref)
    copies[3].wait()
    copies[4].wait()

    def lift(b, carry):
        ks = [b * group + g for g in range(group)]
        x = jnp.concatenate([av[k].reshape(size, levels) for k in ks], axis=1)
        hi, lo = split2(dot(mm[...], x))
        bases = []
        for g in range(group):
            part = slice(g * levels, (g + 1) * levels)
            both = jnp.concatenate([hi[:, part], lo[:, part]], axis=1)
            bases.append(dot_nt(both, lv_nt).reshape(rows, cols, levels))
        for v in range(V):
            total = ens[ks[0], v].astype(F32) * bases[0]
            for g in range(1, group):
                total = total + ens[ks[g], v].astype(F32) * bases[g]
            for s in range(2):
                bi[s, v] += total[2 + s * mid : 2 + (s + 1) * mid]
                b0[s, v] += total[edge[s], half[0]]
                b1[s, v] += total[edge[s], half[1]]
        return carry

    lax.fori_loop(0, members // group, lift, 0)

    def to_mate(g):
        part, rec, rec2, full = stage_refs[g]
        return remote(part.at[1 - p], rec, sh_s.at[g, 0], sh_r.at[g, 0], mate, t)

    def to_peer(g, d):
        part, rec, rec2, full = stage_refs[g]
        return remote(part.at[p], rec2.at[d - 1], sh_s.at[g, d], sh_r.at[g, d], lax.rem(m + 2 * d, n), t)

    def back_to_mate(g):
        part, rec, rec2, full = stage_refs[g]
        return remote(full.at[p], full.at[p], sh_s.at[g, n // 2], sh_r.at[g, n // 2], mate, t)

    def back_from_mate(g):
        part, rec, rec2, full = stage_refs[g]
        return remote(full.at[1 - p], full.at[1 - p], sh_s.at[g, n // 2], sh_r.at[g, n // 2], mate, t)

    def reduce_chip(g):
        part, rec, rec2, full = stage_refs[g]
        to_mate(g).wait_recv()
        part[p] += rec[...]
        for d in range(1, n // 2):
            to_peer(g, d).start()

    def reduce_rest(g):
        part, rec, rec2, full = stage_refs[g]
        total = part[p]
        for d in range(1, n // 2):
            to_peer(g, d).wait_recv()
            total = total + rec2[d - 1]
        full[p] = total

    def outer_copy(h, s, other):
        full = stage_refs[h][3]
        return remote(full.at[s, :, s], ihalo.at[h, 1 - s], ih_s.at[h, s, other], ih_r.at[h, 1 - s],
                      mate if other else m, near[s])

    def outer_recv(h, s):
        return remote(ihalo.at[h, s], ihalo.at[h, s], ih_s.at[h, s, 0], ih_r.at[h, s], m, near[s])

    def outer_send(h):
        for s in range(2):
            @pl.when(has[s] & (p == s))
            def _(s=s):
                outer_copy(h, s, 0).start()
                outer_copy(h, s, 1).start()

    to_mate(2).start()
    first.forward(0, order[0])
    for k in range(5, 9):
        copies[k].wait()

    place = col[...]
    wide = 2 * cols
    frow = lax.div(place, wide)
    fcol = place - frow * wide
    slot = lax.broadcasted_iota(jnp.int32, (1, slots), 1)
    variable = lax.rem(slot, V)
    early = fcol <= 2 * (ch - 1)
    live = slot < cnt[0]

    def weights(fine, count, shift):
        main = lax.div(fine, 2)
        other = jnp.where(fine - 2 * main == 1, main + 1, main - 1)
        at = lax.broadcasted_iota(jnp.int32, (count, slots), 0) - shift
        return jnp.where(at == main, 0.75, 0.0) + jnp.where(at == other, 0.25, 0.0)

    wr = weights(frow, rows + 2, 1)
    wc = weights(fcol, cols, 0)
    w15[...] = jnp.zeros_like(w15)
    for v in range(V):
        mask = jnp.where(variable == v, 1.0, 0.0)
        for a in range(rows + 2):
            start = (a * V + v) * ch
            line = wr[a : a + 1, :] * mask
            for h in range(2):
                wt[h, start : start + ch, :] = (wc[half[h]] * line).astype(BF16)
            w15[a * V + v : a * V + v + 1, :] = wc[ch - 1 : ch] * line
        if v == 0:
            reduce_chip(2)
    for c in order[1:-1]:
        first.forward(0, c)
    reduce_rest(2)
    back_to_mate(2).start()
    first.forward(0, order[-1])

    e15[...] = jnp.zeros_like(e15)
    for s in range(2):
        for w in range(2):
            row = s * (rows - 2) + w
            for v in range(V):
                for k in range(members):
                    e15[s, w, v, k : k + 1, :] = ens[k, v, row, ch - 1 : ch, :].astype(F32)

    def edge_increment(h, c):
        part = stage_refs[h][0]
        sums = [[None] * V for _ in range(2)]
        for k in range(c * per, (c + 1) * per):
            above, below = hr[h, 0, k], hr[h, 1, k]
            fields = (jnp.stack([above[0] + 4.0 * above[1], above[1]]),
                      jnp.stack([below[0], 4.0 * below[0] + below[1]]))
            for s in range(2):
                for v in range(V):
                    term = ens[k, v, edge[s], half[h]].astype(F32) * fields[s]
                    sums[s][v] = term if sums[s][v] is None else sums[s][v] + term
        for s in range(2):
            for v in range(V):
                part[s, v] += sums[s][v]

    def whole(h):
        full = stage_refs[h][3]
        pieces = [ihalo[h, 0], full[0, :, 0], full[0, :, 1]]
        pieces += [fi[s, :, a, half[h]] for s in range(2) for a in range(mid)]
        pieces += [full[1, :, 0], full[1, :, 1], ihalo[h, 1]]
        return jnp.concatenate(pieces, axis=0).reshape(V * (rows + 2) * ch, levels)

    hot = lax.broadcasted_iota(jnp.int32, (levels, slots), 0) == lev[...]

    def pick(h):
        both = jnp.concatenate(split2(whole(h).T), axis=0)
        picked = dot(both, wt[h])
        return jnp.sum(jnp.where(hot, picked[:levels] + picked[levels:], 0.0), axis=0, keepdims=True)

    def spread(weighted):
        hi, lo = split2(jnp.where(hot, jnp.broadcast_to(weighted, hot.shape), 0.0))
        sent[0:levels, :] = hi
        sent[levels:, :] = lo

    def adjoint(h, a, count):
        both = dot_nt(wt[h, a * V * ch : (a + count) * V * ch, :], sent[...])
        return (both[:, :levels] + both[:, levels:]).reshape(count, V, ch, levels)

    def near_copy(src, dst, ssem, rsem, h, s):
        return remote(src.at[h, s], dst.at[h, 1 - s], ssem.at[h, s], rsem.at[h, 1 - s], m, near[s])

    def single_copy(src, dst, ssem, rsem, s):
        return remote(src.at[s], dst.at[1 - s], ssem.at[s], rsem.at[1 - s], m, near[s])

    def adjoint_edges(h):
        top, bottom = adjoint(h, 0, 3), adjoint(h, rows - 1, 3)
        adjs[h, 0] = top[0]
        adjs[h, 1] = bottom[2]
        for s in range(2):
            @pl.when(has[s])
            def _(s=s):
                near_copy(adjs, ahalo, ah_s, ah_r, h, s).start()
        for a in range(2):
            adj[:, a, half[h]] = top[1 + a]
            adj[:, rows - 2 + a, half[h]] = bottom[a]

    def adjoint_halo(h):
        for s in range(2):
            @pl.when(has[s])
            def _(s=s):
                remote(ahalo.at[h, s], ahalo.at[h, s], ah_s.at[h, s], ah_r.at[h, s], m, near[s]).wait_recv()
        adj[:, 0, half[h]] += ahalo[h, 0]
        adj[:, rows - 1, half[h]] += ahalo[h, 1]

    def fields(h, c):
        weights = [[adj[v, edge[s], half[h]] for v in range(V)] for s in range(2)]
        for k in range(c * per, (c + 1) * per):
            for s in range(2):
                total = ens[k, 0, edge[s], half[h]].astype(F32) * weights[s][0]
                for v in range(1, V):
                    total = total + ens[k, v, edge[s], half[h]].astype(F32) * weights[s][v]
                gs[h, s, k] = total

    def chain_sums(h, middle, later):
        to_mate(h).start()
        middle()
        reduce_chip(h)
        reduce_rest(h)
        back_to_mate(h).start()
        outer_send(h)
        later()

    def chain_close(h):
        back_from_mate(h).wait_recv()
        for s in range(2):
            @pl.when(has[s])
            def _(s=s):
                outer_recv(h, s).wait_recv()

    for c in order:
        first.receive(0, c)
        edge_increment(0, c)
    rest = order[chunks // 2 :]

    def after_outer_a():
        for c in rest[:1]:
            first.send(1, c)
        first.forward(1, order[0])

    chain_sums(0, lambda: None, after_outer_a)
    back_from_mate(2).wait_recv()
    chain_close(0)
    value = pick(0)
    weighted = jnp.where(live & early, wgt[...] * (value - innov[...]), 0.0)
    spread(weighted)
    adjoint_edges(0)
    for c in rest[1:]:
        first.send(1, c)
    for c in order[1:]:
        first.forward(1, c)
    adjoint_halo(0)
    for c in order:
        fields(0, c)
        second.send(0, c)

    for c in order:
        first.receive(1, c)
        edge_increment(1, c)
    chain_sums(1, lambda: None, lambda: second.forward(0, order[0]))
    chain_close(1)
    value = value + pick(1)
    spread(jnp.where(live, wgt[...] * (value - innov[...]), 0.0))
    adjoint_edges(1)
    thin = dot_nt(w15[...].astype(BF16), sent[...])
    thin = thin[:, :levels] + thin[:, levels:]
    adjs15[0, 0:V] = thin[0:V]
    adjs15[1, 0:V] = thin[(rows + 1) * V : (rows + 2) * V]
    for s in range(2):
        @pl.when(has[s])
        def _(s=s):
            single_copy(adjs15, ahalo15, a15_s, a15_r, s).start()
    for c in order[1:]:
        second.forward(0, c)
    adjoint_halo(1)
    for s in range(2):
        @pl.when(has[s])
        def _(s=s):
            remote(ahalo15.at[s], ahalo15.at[s], a15_s.at[s], a15_r.at[s], m, near[s]).wait_recv()
    for s in range(2):
        for w in range(2):
            a = 1 + s * (rows - 2) + w
            line = thin[a * V : (a + 1) * V]
            if w == s:
                line = line + ahalo15[s, 0:V]
            total = e15[s, w, 0] * line[0:1]
            for v in range(1, V):
                total = total + e15[s, w, v] * line[v : v + 1]
            gs15[s, w] = total
            for v in range(V):
                adj[v, s * (rows - 2) + w, ch - 1 : ch, :] = line[v : v + 1]
    for c in order:
        fields(1, c)
        second.send(1, c)
        if c == order[0]:
            for s in range(2):
                @pl.when(has[s])
                def _(s=s):
                    single_copy(gs15, gr15, g15_s, g15_r, s).start()
    for h in range(2):
        inner = adjoint(h, 3, rows - 4)
        for a in range(rows - 4):
            adj[:, 2 + a, half[h]] = inner[a]

    pair = 2 if members % 2 == 0 else 1

    def inside(b, carry):
        ks = [b * pair + g for g in range(pair)]
        parts = []
        for k in ks:
            total = ens[k, 0].astype(F32) * adj[0]
            for v in range(1, V):
                total = total + ens[k, v].astype(F32) * adj[v]
            parts.append(total.reshape(size, levels))
        hi, lo = split2(jnp.concatenate(parts, axis=1))
        hi, lo = split2(dot(mm[...], hi) + dot(mm[...], lo))
        for g, k in enumerate(ks):
            part = slice(g * levels, (g + 1) * levels)
            both = jnp.concatenate([hi[:, part], lo[:, part]], axis=1)
            out[k] = av[k].astype(F32) + dot(both, lv_nn).reshape(rows, cols, levels)
        return carry

    first_pairs = (members // pair) // 2
    lax.fori_loop(0, first_pairs, inside, 0)
    for c in order:
        second.forward(1, c)
    lax.fori_loop(first_pairs, members // pair, inside, 0)

    for c in order:
        second.receive(0, c)
    for s in range(2):
        @pl.when(has[s])
        def _(s=s):
            remote(gr15.at[s], gr15.at[s], g15_s.at[s], g15_r.at[s], m, near[s]).wait_recv()

    def outer(k):
        sides = []
        for s in range(2):
            body = jnp.concatenate([gr[0, s, k], gr[1, s, k]], axis=1)
            at = lax.broadcasted_iota(jnp.int32, body.shape, 1)
            line = jnp.stack([gr15[s, w, k : k + 1] for w in range(2)])
            sides.append(jnp.where(at == ch - 1, jnp.broadcast_to(line, body.shape), body))
        around = jnp.concatenate(sides, axis=0).reshape(4 * cols, levels)
        back = dot(em[...], jnp.concatenate(split2(around), axis=0))
        both = jnp.concatenate(split2(back), axis=1)
        add = dot(both, lv_nn).reshape(4, cols, levels)
        out[k, 0:2] += add[0:2]
        out[k, rows - 2 : rows] += add[2:4]

    for c in order:
        second.receive(1, c)
        for k in range(c * per, (c + 1) * per):
            outer(k)

    first.drain()
    second.drain()
    for g in range(3):
        to_mate(g).wait_send()
        for d in range(1, n // 2):
            to_peer(g, d).wait_send()
        back_to_mate(g).wait_send()
    for h in range(2):
        for s in range(2):
            @pl.when(has[s] & (p == s))
            def _(h=h, s=s):
                outer_copy(h, s, 0).wait_send()
                outer_copy(h, s, 1).wait_send()

            @pl.when(has[s])
            def _(h=h, s=s):
                near_copy(adjs, ahalo, ah_s, ah_r, h, s).wait_send()
    for s in range(2):
        @pl.when(has[s])
        def _(s=s):
            single_copy(adjs15, ahalo15, a15_s, a15_r, s).wait_send()
            single_copy(gs15, gr15, g15_s, g15_r, s).wait_send()


def solution(mesh):
    n = mesh.shape["mem"]
    tiles = mesh.shape["tile"]

    def on_device(alpha, ensemble, loc_vert, obs_col, obs_lev, obs_count, innovation, obs_weight):
        members, rows, cols, levels = alpha.shape
        slots = obs_col.shape[1]
        chunks = 4 if members % 4 == 0 else 1
        ch = cols // 2
        mid = (rows - 4) // 2
        vmem = pl.BlockSpec(memory_space=pltpu.VMEM)
        hbm = pl.BlockSpec(memory_space=pltpu.HBM)
        turned = pltpu.VMEM((2, 2, members, 2, ch, levels), F32)
        passing = pltpu.VMEM((2, members, 2, ch, levels), F32)
        dma = pltpu.SemaphoreType.DMA
        line = pltpu.VMEM((1, slots), F32)
        mark = pltpu.VMEM((1, slots), jnp.int32)
        padded = -(-members // 8) * 8
        thin = -(-V * (rows + 2) // 16) * 16

        def sums(piece):
            return [pltpu.VMEM((2,) + piece, F32), pltpu.VMEM(piece, F32),
                    pltpu.VMEM((max(n // 2 - 1, 1),) + piece, F32), pltpu.VMEM((2,) + piece, F32)]

        borders = pltpu.VMEM((2, 2, V, ch, levels), F32)
        small = pltpu.VMEM((2, 8, levels), F32)
        slim = pltpu.VMEM((2, 2, padded, levels), F32)
        return pl.pallas_call(
            functools.partial(kernel, n, tiles, chunks),
            out_shape=jax.ShapeDtypeStruct(alpha.shape, F32),
            in_specs=[hbm, hbm, hbm, hbm, hbm, pl.BlockSpec(memory_space=pltpu.SMEM), hbm, hbm],
            out_specs=vmem,
            scratch_shapes=[
                pltpu.VMEM(alpha.shape, BF16), pltpu.VMEM(ensemble.shape, BF16),
                pltpu.VMEM(loc_vert.shape, BF16), mark, mark, line, line,
                turned, turned, passing, turned, turned, passing,
                pltpu.VMEM((rows * cols, rows * cols), BF16),
                pltpu.VMEM((4 * cols, 4 * cols), BF16),
                pltpu.VMEM((4 * cols, 8 * cols), BF16),
                pltpu.VMEM((2, V * (rows + 2) * ch, slots), BF16),
                pltpu.VMEM((thin, slots), F32),
                pltpu.VMEM((2 * levels, slots), BF16),
                pltpu.VMEM((2, 2, V, padded, levels), F32),
                *sums((V, mid, cols, levels)), *sums((V, 2, ch, levels)), *sums((V, 2, ch, levels)),
                borders, pltpu.VMEM((V, rows, cols, levels), F32), borders, borders,
                small, small, slim, slim,
                dma((9,)),
                dma((2, 2, chunks)), dma((2, 2, chunks)), dma((2, chunks)), dma((2, chunks)),
                dma((2, 2, chunks)), dma((2, 2, chunks)), dma((2, chunks)), dma((2, chunks)),
                dma((3, n // 2 + 1)), dma((3, n // 2 + 1)),
                dma((2, 2, 2)), dma((2, 2)), dma((2, 2)), dma((2, 2)),
                dma((2,)), dma((2,)), dma((2,)), dma((2,)),
            ],
            compiler_params=pltpu.CompilerParams(
                collective_id=0, has_side_effects=True, vmem_limit_bytes=58 << 20),
        )(alpha, ensemble, loc_vert, obs_col, obs_lev, obs_count, innovation, obs_weight)

    in_specs = (
        P("mem", "tile", None, None),
        P("mem", None, "tile", None, None),
        P(),
        P("tile", None),
        P("tile", None),
        P("tile"),
        P("tile", None),
        P("tile", None),
    )
    out_specs = P("mem", "tile", None, None)
    return jax.shard_map(
        on_device, mesh=mesh, in_specs=in_specs, out_specs=out_specs, check_vma=False
    )
```

time: 88.1 us -> 79.9 us (0.907)
  the two profiles are of different devices: /device:TPU:16 before, /device:TPU:0 now
where the time goes in v1:
time: 79.9 us; the launch traced here: 79.7 us
  Pallas kernels  75.5 us (94%)
  local copies, waits for them, and re-layouts  3.57 us (4%)
    pallas_call x1, Pallas kernels, on_device(): pl.pallas_call(functools.partial(kernel, n, tiles, chunks), out_shape=jax...  75.5 us
    unnamed x1, local copies, waits for them, and re-layouts  3.57 us

profile of v1, /device:TPU:0, one launch (start us, length us, event | category | flops | bytes accessed | tf_op | source)
XLA Modules:
  0.0 79.7 jit_solution(4582795375895918145)
XLA Ops:
  0.7 75.5 %shard_map.82 = f32[20,8,32,128]{3,2,1,0:T(8,128)} custom-call(bf16[20,8,32,128]{3,2,1,0:T(8,128)(2,1)} %alpha_h.1, bf16[20,3,8,32,128]{4,3,2,1,0:T(8,128)(2,1)} %ens_h.1, bf16[128,128]{1,0:T(8,128)(2,1)} %loc_h.1, s32[1,2048]{1,0:T(1,128)} %col_h.1, s32[1,2048]{1,0:T(1,128)} %lev_h.1, s32[1]{0:T(128)S(6)} %copy.10.cnt, f32[1,2048]{1,0:T(1,128)} %innov_h.1, ...), custom_call_target="tpu_custom_call" | custom-call | tf_op jit(solution)/shard_map/pallas_call | solution.py:623
  76.1 3.6 %copy.11 = f32[20,8,32,128]{3,2,1,0:T(8,128)} copy(f32[20,8,32,128]{3,2,1,0:T(8,128)} %shard_map.82) | data formatting | bytes 5242880

commit v2 on v1

--- a/solution.py
+++ b/solution.py
@@ -41,7 +41,7 @@
            av, ens, loc, col, lev, innov, wgt,
            hs, hr, hl, gs, gr, gl, mm, sc, em, wt, w15, sent, e15,
            bi, bi1, bi2, fi, b0, b01, b02, f0, b1, b11, b12, f1,
-           ihalo, adj, adjs, ahalo, adjs15, ahalo15, gs15, gr15,
+           iy, adj, adjs, ahalo, adjs15, ahalo15, gs15, gr15,
            in_sem, hs_s, hs_r, hl_s, hl_r, gs_s, gs_r, gl_s, gl_r,
            sh_s, sh_r, ih_s, ih_r, ah_s, ah_r, a15_s, a15_r, g15_s, g15_r):
     members, rows, cols, levels = out.shape
@@ -95,9 +95,9 @@
     for s in range(2):
         @pl.when(has[s])
         def _(s=s):
-            greet(m, near[s])
-            greet(mate, near[s])
-        total = total + 2 * has[s].astype(jnp.int32)
+            for d in range(n // 2):
+                greet(lax.rem(m + 2 * d, n), near[s])
+        total = total + (n // 2) * has[s].astype(jnp.int32)
         if relays:
             @pl.when(far[s])
             def _(s=s):
@@ -129,22 +129,33 @@
             return remote(self.via.at[h, part], self.dst.at[h, odd, part],
                           self.vs.at[h, c], self.sr.at[h, odd, c], m, t + 2 - 4 * odd)
 
-        def send(self, h, c):
+        def send_turned(self, h, c):
             for s in range(2):
                 if relays:
-                    turned = (odd == s) & (c >= chunks - n_out)
-
-                    @pl.when(has[s] & turned)
+                    @pl.when(has[s] & (odd == s) & (c >= chunks - n_out))
                     def _(s=s):
                         self.detour(h, s, c).start()
 
-                    @pl.when(has[s] & jnp.logical_not(turned))
-                    def _(s=s):
-                        self.direct(h, s, c).start()
-                else:
-                    @pl.when(has[s])
-                    def _(s=s):
-                        self.direct(h, s, c).start()
+        def send_far(self, h, c):
+            for s in range(2):
+                straight = c < chunks - n_out if relays else True
+
+                @pl.when(has[s] & (odd == s) & straight)
+                def _(s=s):
+                    self.direct(h, s, c).start()
+
+        def send_near(self, h, c):
+            for s in range(2):
+                @pl.when(has[s] & (odd != s))
+                def _(s=s):
+                    self.direct(h, s, c).start()
+
+        def send(self, h):
+            for c in order:
+                self.send_turned(h, c)
+            for c in order:
+                self.send_far(h, c)
+                self.send_near(h, c)
 
         def forward(self, h, c):
             if relays:
@@ -167,7 +178,7 @@
                            self.ss.at[h, s, c], self.sr.at[h, s, c], m, near[s]).wait_recv()
 
         def drain(self):
-            for h in range(2):
+            for h in range(self.src.shape[0]):
                 for c in range(chunks):
                     for s in range(2):
                         @pl.when(has[s])
@@ -214,17 +225,17 @@
         if not entered:
             pl.semaphore_wait(barrier, total)
             entered = True
-        first.send(0, c)
-    for c in order[: chunks // 2]:
-        first.send(1, c)
+        first.send_turned(0, c)
+        first.send_far(0, c)
+    for c in order:
+        first.send_near(0, c)
+    for c in order:
+        first.send_turned(1, c)
     for s in range(2):
         @pl.when(jnp.logical_not(has[s]))
         def _(s=s):
-            for ref in (hr, gr):
-                for h in range(2):
-                    ref[h, s] = jnp.zeros(ref.shape[2:], F32)
-            for ref in (ihalo, ahalo):
-                for h in range(2):
+            for ref in (hr, gr, ahalo):
+                for h in range(ref.shape[0]):
                     ref[h, s] = jnp.zeros(ref.shape[2:], F32)
             ahalo15[s] = jnp.zeros(ahalo15.shape[1:], F32)
             gr15[s] = jnp.zeros(gr15.shape[1:], F32)
@@ -292,22 +303,34 @@
         for d in range(1, n // 2):
             to_peer(g, d).wait_recv()
             total = total + rec2[d - 1]
-        full[p] = total
-
-    def outer_copy(h, s, other):
-        full = stage_refs[h][3]
-        return remote(full.at[s, :, s], ihalo.at[h, 1 - s], ih_s.at[h, s, other], ih_r.at[h, 1 - s],
-                      mate if other else m, near[s])
-
-    def outer_recv(h, s):
-        return remote(ihalo.at[h, s], ihalo.at[h, s], ih_s.at[h, s, 0], ih_r.at[h, s], m, near[s])
+        return total
+
+    def outer_copy(h, s, d):
+        here = lax.div(m, 2)
+        return remote(stage_refs[h][0].at[p, :, s], iy.at[h, here], ih_s.at[h, d], ih_r.at[h, here],
+                      lax.rem(m + 2 * d, n), near[s])
 
     def outer_send(h):
         for s in range(2):
             @pl.when(has[s] & (p == s))
             def _(s=s):
-                outer_copy(h, s, 0).start()
-                outer_copy(h, s, 1).start()
+                for d in range(n // 2):
+                    outer_copy(h, s, d).start()
+
+    def outer_recv(h):
+        full = stage_refs[h][3]
+        for s in range(2):
+            @pl.when(has[1 - s] & (p == s))
+            def _(s=s):
+                total = None
+                for d in range(n // 2):
+                    remote(iy.at[h, d], iy.at[h, d], ih_s.at[h, 0], ih_r.at[h, d], m, near[1 - s]).wait_recv()
+                    total = iy[h, d] if total is None else total + iy[h, d]
+                full[s, :, 2] = total
+
+            @pl.when(jnp.logical_not(has[1 - s]) & (p == s))
+            def _(s=s):
+                full[s, :, 2] = jnp.zeros(full.shape[1:2] + full.shape[3:], F32)
 
     to_mate(2).start()
     first.forward(0, order[0])
@@ -331,22 +354,29 @@
 
     wr = weights(frow, rows + 2, 1)
     wc = weights(fcol, cols, 0)
+    head = w15.shape[0]
     w15[...] = jnp.zeros_like(w15)
+    rim = [0, 1, 2, rows - 1, rows, rows + 1]
+    lines = rim + list(range(3, rows - 1))
+    cut = head + len(rim) * V * ch
     for v in range(V):
         mask = jnp.where(variable == v, 1.0, 0.0)
-        for a in range(rows + 2):
-            start = (a * V + v) * ch
+        for b, a in enumerate(lines):
+            start = head + (b * V + v) * ch
             line = wr[a : a + 1, :] * mask
             for h in range(2):
                 wt[h, start : start + ch, :] = (wc[half[h]] * line).astype(BF16)
-            w15[a * V + v : a * V + v + 1, :] = wc[ch - 1 : ch] * line
+            if b < len(rim):
+                w15[b * V + v : b * V + v + 1, :] = wc[ch - 1 : ch] * line
         if v == 0:
             reduce_chip(2)
-    for c in order[1:-1]:
+    wt[1, 0:head, :] = w15[...].astype(BF16)
+    for c in order:
+        first.send_far(1, c)
+    for c in order[1:2]:
         first.forward(0, c)
-    reduce_rest(2)
+    fi[p] = reduce_rest(2)
     back_to_mate(2).start()
-    first.forward(0, order[-1])
 
     e15[...] = jnp.zeros_like(e15)
     for s in range(2):
@@ -371,28 +401,32 @@
             for v in range(V):
                 part[s, v] += sums[s][v]
 
-    def whole(h):
+    hot = lax.broadcasted_iota(jnp.int32, (levels, slots), 0) == lev[...]
+
+    def pick(h, pieces, start):
+        flat = jnp.concatenate(pieces, axis=0).reshape(-1, levels)
+        both = jnp.concatenate(split2(flat.T), axis=0)
+        picked = dot(both, wt[h, start : start + flat.shape[0]])
+        return jnp.sum(jnp.where(hot, picked[:levels] + picked[levels:], 0.0), axis=0, keepdims=True)
+
+    def pick_inner(h):
+        return pick(h, [fi[s, :, a, half[h]] for s in range(2) for a in range(mid)], cut)
+
+    def pick_rim(h):
         full = stage_refs[h][3]
-        pieces = [ihalo[h, 0], full[0, :, 0], full[0, :, 1]]
-        pieces += [fi[s, :, a, half[h]] for s in range(2) for a in range(mid)]
-        pieces += [full[1, :, 0], full[1, :, 1], ihalo[h, 1]]
-        return jnp.concatenate(pieces, axis=0).reshape(V * (rows + 2) * ch, levels)
-
-    hot = lax.broadcasted_iota(jnp.int32, (levels, slots), 0) == lev[...]
-
-    def pick(h):
-        both = jnp.concatenate(split2(whole(h).T), axis=0)
-        picked = dot(both, wt[h])
-        return jnp.sum(jnp.where(hot, picked[:levels] + picked[levels:], 0.0), axis=0, keepdims=True)
+        return pick(h, [full[1, :, 2], full[0, :, 0], full[0, :, 1], full[1, :, 0], full[1, :, 1], full[0, :, 2]], head)
 
     def spread(weighted):
         hi, lo = split2(jnp.where(hot, jnp.broadcast_to(weighted, hot.shape), 0.0))
         sent[0:levels, :] = hi
         sent[levels:, :] = lo
 
-    def adjoint(h, a, count):
-        both = dot_nt(wt[h, a * V * ch : (a + count) * V * ch, :], sent[...])
-        return (both[:, :levels] + both[:, levels:]).reshape(count, V, ch, levels)
+    def adjoint(h, start, stop):
+        both = dot_nt(wt[h, start:stop, :], sent[...])
+        return both[:, :levels] + both[:, levels:]
+
+    def shaped(x):
+        return x.reshape(x.shape[0] // (V * ch), V, ch, levels)
 
     def near_copy(src, dst, ssem, rsem, h, s):
         return remote(src.at[h, s], dst.at[h, 1 - s], ssem.at[h, s], rsem.at[h, 1 - s], m, near[s])
@@ -401,16 +435,24 @@
         return remote(src.at[s], dst.at[1 - s], ssem.at[s], rsem.at[1 - s], m, near[s])
 
     def adjoint_edges(h):
-        top, bottom = adjoint(h, 0, 3), adjoint(h, rows - 1, 3)
-        adjs[h, 0] = top[0]
-        adjs[h, 1] = bottom[2]
+        flat = adjoint(h, head * (1 - h), cut)
+        thin = flat[:head] if h else None
+        rims = shaped(flat[head * h :])
+        adjs[h, 0] = rims[0]
+        adjs[h, 1] = rims[5]
+        if h:
+            adjs15[0, 0:V] = thin[0:V]
+            adjs15[1, 0:V] = thin[5 * V : 6 * V]
         for s in range(2):
             @pl.when(has[s])
             def _(s=s):
                 near_copy(adjs, ahalo, ah_s, ah_r, h, s).start()
+                if h:
+                    single_copy(adjs15, ahalo15, a15_s, a15_r, s).start()
         for a in range(2):
-            adj[:, a, half[h]] = top[1 + a]
-            adj[:, rows - 2 + a, half[h]] = bottom[a]
+            adj[:, a, half[h]] = rims[1 + a]
+            adj[:, rows - 2 + a, half[h]] = rims[3 + a]
+        return thin
 
     def adjoint_halo(h):
         for s in range(2):
@@ -420,83 +462,80 @@
         adj[:, 0, half[h]] += ahalo[h, 0]
         adj[:, rows - 1, half[h]] += ahalo[h, 1]
 
-    def fields(h, c):
-        weights = [[adj[v, edge[s], half[h]] for v in range(V)] for s in range(2)]
-        for k in range(c * per, (c + 1) * per):
+    def fields(h, outermost):
+        where = (0, rows - 1) if outermost else (1, rows - 2)
+        weights = [[adj[v, where[s], half[h]] for v in range(V)] for s in range(2)]
+        for k in range(members):
             for s in range(2):
-                total = ens[k, 0, edge[s], half[h]].astype(F32) * weights[s][0]
+                total = ens[k, 0, where[s], half[h]].astype(F32) * weights[s][0]
                 for v in range(1, V):
-                    total = total + ens[k, v, edge[s], half[h]].astype(F32) * weights[s][v]
-                gs[h, s, k] = total
-
-    def chain_sums(h, middle, later):
+                    total = total + ens[k, v, where[s], half[h]].astype(F32) * weights[s][v]
+                gs[2 * h + outermost, s, k] = total
+
+    def chain_open(h):
+        for c in order:
+            first.receive(h, c)
+            edge_increment(h, c)
         to_mate(h).start()
-        middle()
         reduce_chip(h)
-        reduce_rest(h)
+        outer_send(h)
+
+    def chain_close(h):
+        full = stage_refs[h][3]
+        full[p, :, 0:2] = reduce_rest(h)
+        outer_recv(h)
         back_to_mate(h).start()
-        outer_send(h)
-        later()
-
-    def chain_close(h):
         back_from_mate(h).wait_recv()
-        for s in range(2):
-            @pl.when(has[s])
-            def _(s=s):
-                outer_recv(h, s).wait_recv()
-
-    for c in order:
-        first.receive(0, c)
-        edge_increment(0, c)
-    rest = order[chunks // 2 :]
-
-    def after_outer_a():
-        for c in rest[:1]:
-            first.send(1, c)
-        first.forward(1, order[0])
-
-    chain_sums(0, lambda: None, after_outer_a)
+
     back_from_mate(2).wait_recv()
+    value = pick_inner(0)
+    for c in order[2:]:
+        first.forward(0, c)
+    value = value + pick_inner(1)
+
+    chain_open(0)
+    for c in order:
+        first.send_near(1, c)
     chain_close(0)
-    value = pick(0)
+    for c in order[:2]:
+        first.forward(1, c)
+    value = value + pick_rim(0)
     weighted = jnp.where(live & early, wgt[...] * (value - innov[...]), 0.0)
     spread(weighted)
     adjoint_edges(0)
-    for c in rest[1:]:
-        first.send(1, c)
-    for c in order[1:]:
+    fields(0, 0)
+    second.send(0)
+    for c in order[2:]:
         first.forward(1, c)
+
+    chain_open(1)
     adjoint_halo(0)
-    for c in order:
-        fields(0, c)
-        second.send(0, c)
-
-    for c in order:
-        first.receive(1, c)
-        edge_increment(1, c)
-    chain_sums(1, lambda: None, lambda: second.forward(0, order[0]))
+    fields(0, 1)
+    second.send(1)
+    for c in order:
+        second.forward(0, c)
     chain_close(1)
-    value = value + pick(1)
+    value = value + pick_rim(1)
     spread(jnp.where(live, wgt[...] * (value - innov[...]), 0.0))
-    adjoint_edges(1)
-    thin = dot_nt(w15[...].astype(BF16), sent[...])
-    thin = thin[:, :levels] + thin[:, levels:]
-    adjs15[0, 0:V] = thin[0:V]
-    adjs15[1, 0:V] = thin[(rows + 1) * V : (rows + 2) * V]
-    for s in range(2):
-        @pl.when(has[s])
-        def _(s=s):
-            single_copy(adjs15, ahalo15, a15_s, a15_r, s).start()
-    for c in order[1:]:
-        second.forward(0, c)
+    thin = adjoint_edges(1)
+    fields(1, 0)
+    second.send(2)
+    for c in order:
+        second.forward(1, c)
+    for h in range(2):
+        inner = shaped(adjoint(h, cut, wt.shape[1]))
+        for a in range(rows - 4):
+            adj[:, 2 + a, half[h]] = inner[a]
     adjoint_halo(1)
+    fields(1, 1)
+    second.send(3)
     for s in range(2):
         @pl.when(has[s])
         def _(s=s):
             remote(ahalo15.at[s], ahalo15.at[s], a15_s.at[s], a15_r.at[s], m, near[s]).wait_recv()
     for s in range(2):
         for w in range(2):
-            a = 1 + s * (rows - 2) + w
+            a = 1 + 2 * s + w
             line = thin[a * V : (a + 1) * V]
             if w == s:
                 line = line + ahalo15[s, 0:V]
@@ -506,19 +545,10 @@
             gs15[s, w] = total
             for v in range(V):
                 adj[v, s * (rows - 2) + w, ch - 1 : ch, :] = line[v : v + 1]
-    for c in order:
-        fields(1, c)
-        second.send(1, c)
-        if c == order[0]:
-            for s in range(2):
-                @pl.when(has[s])
-                def _(s=s):
-                    single_copy(gs15, gr15, g15_s, g15_r, s).start()
-    for h in range(2):
-        inner = adjoint(h, 3, rows - 4)
-        for a in range(rows - 4):
-            adj[:, 2 + a, half[h]] = inner[a]
-
+    for s in range(2):
+        @pl.when(has[s])
+        def _(s=s):
+            single_copy(gs15, gr15, g15_s, g15_r, s).start()
     pair = 2 if members % 2 == 0 else 1
 
     def inside(b, carry):
@@ -537,23 +567,31 @@
             out[k] = av[k].astype(F32) + dot(both, lv_nn).reshape(rows, cols, levels)
         return carry
 
-    first_pairs = (members // pair) // 2
-    lax.fori_loop(0, first_pairs, inside, 0)
-    for c in order:
-        second.forward(1, c)
-    lax.fori_loop(first_pairs, members // pair, inside, 0)
-
-    for c in order:
-        second.receive(0, c)
+    steps = members // pair
+    stops = [0, steps // 5, 2 * steps // 5, steps]
+    lax.fori_loop(stops[0], stops[1], inside, 0)
+    for c in order[:2]:
+        second.forward(2, c)
+    lax.fori_loop(stops[1], stops[2], inside, 0)
+    for c in order[2:]:
+        second.forward(2, c)
+    lax.fori_loop(stops[2], stops[3], inside, 0)
+    for c in order:
+        second.forward(3, c)
+
     for s in range(2):
         @pl.when(has[s])
         def _(s=s):
             remote(gr15.at[s], gr15.at[s], g15_s.at[s], g15_r.at[s], m, near[s]).wait_recv()
+    for g in range(3):
+        for c in order:
+            second.receive(g, c)
 
     def outer(k):
         sides = []
         for s in range(2):
-            body = jnp.concatenate([gr[0, s, k], gr[1, s, k]], axis=1)
+            turn_rows = (0, 1) if s == 0 else (1, 0)
+            body = jnp.stack([jnp.concatenate([gr[o, s, k], gr[2 + o, s, k]], axis=0) for o in turn_rows])
             at = lax.broadcasted_iota(jnp.int32, body.shape, 1)
             line = jnp.stack([gr15[s, w, k : k + 1] for w in range(2)])
             sides.append(jnp.where(at == ch - 1, jnp.broadcast_to(line, body.shape), body))
@@ -565,7 +603,7 @@
         out[k, rows - 2 : rows] += add[2:4]
 
     for c in order:
-        second.receive(1, c)
+        second.receive(3, c)
         for k in range(c * per, (c + 1) * per):
             outer(k)
 
@@ -580,8 +618,8 @@
         for s in range(2):
             @pl.when(has[s] & (p == s))
             def _(h=h, s=s):
-                outer_copy(h, s, 0).wait_send()
-                outer_copy(h, s, 1).wait_send()
+                for d in range(n // 2):
+                    outer_copy(h, s, d).wait_send()
 
             @pl.when(has[s])
             def _(h=h, s=s):
@@ -607,15 +645,17 @@
         hbm = pl.BlockSpec(memory_space=pltpu.HBM)
         turned = pltpu.VMEM((2, 2, members, 2, ch, levels), F32)
         passing = pltpu.VMEM((2, members, 2, ch, levels), F32)
+        line2 = pltpu.VMEM((4, 2, members, ch, levels), F32)
+        passing2 = pltpu.VMEM((4, members, ch, levels), F32)
         dma = pltpu.SemaphoreType.DMA
         line = pltpu.VMEM((1, slots), F32)
         mark = pltpu.VMEM((1, slots), jnp.int32)
         padded = -(-members // 8) * 8
-        thin = -(-V * (rows + 2) // 16) * 16
-
-        def sums(piece):
+        thin = -(-6 * V // 16) * 16
+
+        def sums(piece, result):
             return [pltpu.VMEM((2,) + piece, F32), pltpu.VMEM(piece, F32),
-                    pltpu.VMEM((max(n // 2 - 1, 1),) + piece, F32), pltpu.VMEM((2,) + piece, F32)]
+                    pltpu.VMEM((max(n // 2 - 1, 1),) + piece, F32), pltpu.VMEM((2,) + result, F32)]
 
         borders = pltpu.VMEM((2, 2, V, ch, levels), F32)
         small = pltpu.VMEM((2, 8, levels), F32)
@@ -628,27 +668,29 @@
             scratch_shapes=[
                 pltpu.VMEM(alpha.shape, BF16), pltpu.VMEM(ensemble.shape, BF16),
                 pltpu.VMEM(loc_vert.shape, BF16), mark, mark, line, line,
-                turned, turned, passing, turned, turned, passing,
+                turned, turned, passing, line2, line2, passing2,
                 pltpu.VMEM((rows * cols, rows * cols), BF16),
                 pltpu.VMEM((4 * cols, 4 * cols), BF16),
                 pltpu.VMEM((4 * cols, 8 * cols), BF16),
-                pltpu.VMEM((2, V * (rows + 2) * ch, slots), BF16),
+                pltpu.VMEM((2, thin + V * (rows + 2) * ch, slots), BF16),
                 pltpu.VMEM((thin, slots), F32),
                 pltpu.VMEM((2 * levels, slots), BF16),
                 pltpu.VMEM((2, 2, V, padded, levels), F32),
-                *sums((V, mid, cols, levels)), *sums((V, 2, ch, levels)), *sums((V, 2, ch, levels)),
-                borders, pltpu.VMEM((V, rows, cols, levels), F32), borders, borders,
+                *sums((V, mid, cols, levels), (V, mid, cols, levels)),
+                *sums((V, 2, ch, levels), (V, 3, ch, levels)), *sums((V, 2, ch, levels), (V, 3, ch, levels)),
+                pltpu.VMEM((2, n // 2, V, ch, levels), F32), pltpu.VMEM((V, rows, cols, levels), F32), borders, borders,
                 small, small, slim, slim,
                 dma((9,)),
                 dma((2, 2, chunks)), dma((2, 2, chunks)), dma((2, chunks)), dma((2, chunks)),
-                dma((2, 2, chunks)), dma((2, 2, chunks)), dma((2, chunks)), dma((2, chunks)),
+                dma((4, 2, chunks)), dma((4, 2, chunks)), dma((4, chunks)), dma((4, chunks)),
                 dma((3, n // 2 + 1)), dma((3, n // 2 + 1)),
-                dma((2, 2, 2)), dma((2, 2)), dma((2, 2)), dma((2, 2)),
+                dma((2, n // 2)), dma((2, n // 2)), dma((2, 2)), dma((2, 2)),
                 dma((2,)), dma((2,)), dma((2,)), dma((2,)),
             ],
             compiler_params=pltpu.CompilerParams(
-                collective_id=0, has_side_effects=True, vmem_limit_bytes=58 << 20),
-        )(alpha, ensemble, loc_vert, obs_col, obs_lev, obs_count, innovation, obs_weight)
+                collective_id=0, has_side_effects=True, vmem_limit_bytes=48 << 20),
+        )(*[pltpu.with_memory_space_constraint(x, pltpu.HBM) for x in (alpha, ensemble, loc_vert, obs_col, obs_lev)],
+          obs_count, *[pltpu.with_memory_space_constraint(x, pltpu.HBM) for x in (innovation, obs_weight)])
 
     in_specs = (
         P("mem", "tile", None, None),

time: 79.9 us -> 68.3 us (0.85)
  Pallas kernels: 75.5 us -> 66 us
  local copies, waits for them, and re-layouts: 3.57 us -> 1.49 us
    pallas_call x1, Pallas kernels: 75.5 us -> 66 us  [on_device(): pl.pallas_call(functools.partial(kernel, n, tiles, chunks), out_shape=jax...]
    unnamed x1, local copies, waits for them, and re-layouts: 3.57 us -> 1.49 us
where the time goes in v2:
time: 68.3 us; the launch traced here: 68.1 us
  Pallas kernels  66 us (97%)
  local copies, waits for them, and re-layouts  1.49 us (2%)
    pallas_call x1, Pallas kernels, on_device(): pl.pallas_call(functools.partial(kernel, n, tiles, chunks), out_shape=jax...  66 us
    unnamed x1, local copies, waits for them, and re-layouts  1.49 us

profile of v2, /device:TPU:0, one launch (start us, length us, event | category | flops | bytes accessed | tf_op | source)
XLA Modules:
  0.0 68.1 jit_solution(15408961770564418562)
XLA Ops:
  0.7 66.0 %shard_map.82 = f32[20,8,32,128]{3,2,1,0:T(8,128)S(1)} custom-call(bf16[20,8,32,128]{3,2,1,0:T(8,128)(2,1)} %alpha_h.1, bf16[20,3,8,32,128]{4,3,2,1,0:T(8,128)(2,1)} %ens_h.1, bf16[128,128]{1,0:T(8,128)(2,1)} %loc_h.1, s32[1,2048]{1,0:T(1,128)} %col_h.1, s32[1,2048]{1,0:T(1,128)} %lev_h.1, s32[1]{0:T(128)S(6)} %copy.10.cnt, f32[1,2048]{1,0:T(1,128)} %innov_h.1, ...), custom_call_target="tpu_custom_call" | custom-call | tf_op jit(solution)/shard_map/pallas_call | solution.py:663
  66.6 1.5 %copy.11 = f32[20,8,32,128]{3,2,1,0:T(8,128)} copy(f32[20,8,32,128]{3,2,1,0:T(8,128)S(1)} %shard_map.82) | data formatting | bytes 5242880

commit v3 on v2

--- a/solution.py
+++ b/solution.py
@@ -42,8 +42,8 @@
            hs, hr, hl, gs, gr, gl, mm, sc, em, wt, w15, sent, e15,
            bi, bi1, bi2, fi, b0, b01, b02, f0, b1, b11, b12, f1,
            iy, adj, adjs, ahalo, adjs15, ahalo15, gs15, gr15,
-           in_sem, hs_s, hs_r, hl_s, hl_r, gs_s, gs_r, gl_s, gl_r,
-           sh_s, sh_r, ih_s, ih_r, ah_s, ah_r, a15_s, a15_r, g15_s, g15_r):
+           in_sem, hs_s, hs_r, hl_s, hl_r, gs_s, gs_r, ge_r, gl_s, gl_r,
+           sh_s, sh_r, ih_s, ih_r, ah_s, ah_r, ah_f, a15_s, a15_r, g15_s, g15_r):
     members, rows, cols, levels = out.shape
     size = rows * cols
     ch = cols // 2
@@ -75,6 +75,7 @@
         copy.start()
 
     relays = tiles % 2 == 0 and tiles >= 4
+    lead = chunks // 2
     odd = lax.rem(t, 2)
     turn = tiles // 2
     share_out = lax.div(chunks * lax.div(t + odd, 2), max(turn, 1))
@@ -110,24 +111,40 @@
             device_id={"mem": who, "tile": where}, device_id_type=MESH)
 
     class Halo:
-        def __init__(self, src, dst, via, ss, sr, vs, vr):
+        def __init__(self, src, dst, via, ss, sr, vs, vr, groups, fine=None):
             self.src, self.dst, self.via = src, dst, via
             self.ss, self.sr, self.vs, self.vr = ss, sr, vs, vr
+            self.groups, self.fine = groups, fine
+
+        def group(self, h):
+            return [b for b, span in enumerate(self.groups) if span[0] <= h < span[1]][0]
+
+        def landed(self, h, s, c):
+            if self.fine is not None and h == self.src.shape[0] - 1:
+                return self.fine.at[s, c]
+            return self.sr.at[self.group(h), s]
 
         def direct(self, h, s, c):
             part = pl.ds(c * per, per)
             return remote(self.src.at[h, s, part], self.dst.at[h, 1 - s, part],
-                          self.ss.at[h, s, c], self.sr.at[h, 1 - s, c], m, near[s])
+                          self.ss.at[s], self.landed(h, 1 - s, c), m, near[s])
+
+        def receive_chunk(self, h, c):
+            for s in range(2):
+                @pl.when(has[s])
+                def _(s=s):
+                    part = self.dst.at[h, s, pl.ds(c * per, per)]
+                    remote(part, part, self.ss.at[s], self.landed(h, s, c), m, near[s]).wait_recv()
 
         def detour(self, h, s, c):
             part = pl.ds(c * per, per)
             return remote(self.src.at[h, s, part], self.via.at[h, part],
-                          self.ss.at[h, s, c], self.vr.at[h, c], m, t + 1 - 2 * odd)
+                          self.ss.at[s], self.vr.at[h, c], m, t + 1 - 2 * odd)
 
         def onward(self, h, c):
             part = pl.ds(c * per, per)
             return remote(self.via.at[h, part], self.dst.at[h, odd, part],
-                          self.vs.at[h, c], self.sr.at[h, odd, c], m, t + 2 - 4 * odd)
+                          self.vs.at[0], self.landed(h, odd, c), m, t + 2 - 4 * odd)
 
         def send_turned(self, h, c):
             for s in range(2):
@@ -144,17 +161,16 @@
                 def _(s=s):
                     self.direct(h, s, c).start()
 
-        def send_near(self, h, c):
-            for s in range(2):
-                @pl.when(has[s] & (odd != s))
+        def send_near(self, h, c, when=True):
+            for s in range(2):
+                @pl.when(has[s] & (odd != s) & when)
                 def _(s=s):
                     self.direct(h, s, c).start()
 
-        def send(self, h):
+        def send_close(self, h):
             for c in order:
                 self.send_turned(h, c)
             for c in order:
-                self.send_far(h, c)
                 self.send_near(h, c)
 
         def forward(self, h, c):
@@ -167,30 +183,30 @@
         def onward_recv(self, h, c):
             part = pl.ds(c * per, per)
             return remote(self.via.at[h, part], self.via.at[h, part],
-                          self.vs.at[h, c], self.vr.at[h, c], m, t + 1 - 2 * odd)
-
-        def receive(self, h, c):
+                          self.vs.at[0], self.vr.at[h, c], m, t + 1 - 2 * odd)
+
+        def receive(self, b):
+            span = self.groups[b]
             for s in range(2):
                 @pl.when(has[s])
                 def _(s=s):
-                    part = pl.ds(c * per, per)
-                    remote(self.dst.at[h, s, part], self.dst.at[h, s, part],
-                           self.ss.at[h, s, c], self.sr.at[h, s, c], m, near[s]).wait_recv()
+                    every = self.dst.at[span[0] : span[1], s]
+                    remote(every, every, self.ss.at[s], self.sr.at[b, s], m, near[s]).wait_recv()
 
         def drain(self):
-            for h in range(self.src.shape[0]):
-                for c in range(chunks):
-                    for s in range(2):
-                        @pl.when(has[s])
-                        def _(h=h, s=s, c=c):
-                            self.direct(h, s, c).wait_send()
-                    if relays:
-                        @pl.when(passes & (c >= chunks - n_in))
-                        def _(h=h, c=c):
-                            self.onward(h, c).wait_send()
-
-    first = Halo(hs, hr, hl, hs_s, hs_r, hl_s, hl_r)
-    second = Halo(gs, gr, gl, gs_s, gs_r, gl_s, gl_r)
+            for s in range(2):
+                @pl.when(has[s])
+                def _(s=s):
+                    remote(self.src.at[:, s], self.dst.at[:, s], self.ss.at[s], self.sr.at[0, s], m, near[s]).wait_send()
+            if relays:
+                for count in range(1, chunks + 1):
+                    @pl.when(passes & (n_in == count))
+                    def _(count=count):
+                        every = self.via.at[:, members - count * per : members]
+                        remote(every, every, self.vs.at[0], self.sr.at[0, 0], m, t + 2 - 4 * odd).wait_send()
+
+    first = Halo(hs, hr, hl, hs_s, hs_r, hl_s, hl_r, ((0, 1), (1, 2)))
+    second = Halo(gs, gr, gl, gs_s, gs_r, gl_s, gl_r, ((0, 3),), ge_r)
     order = list(range(chunks - 1, -1, -1))
 
     i = lax.broadcasted_iota(jnp.int32, (4 * cols, 4 * cols), 0)
@@ -218,19 +234,21 @@
             for h in range(2):
                 hs[h, s, k] = u[2 * s : 2 * s + 2, half[h]]
 
-    entered = False
     for c in order:
         for k in range(c * per, (c + 1) * per):
             prepare(k)
-        if not entered:
+        if c == order[0]:
             pl.semaphore_wait(barrier, total)
-            entered = True
         first.send_turned(0, c)
         first.send_far(0, c)
-    for c in order:
-        first.send_near(0, c)
+        if c != order[0]:
+            first.send_near(0, c + 1)
+    first.send_near(0, order[-1])
     for c in order:
         first.send_turned(1, c)
+    ahead = [(chunks - c) + n_out <= lead for c in range(chunks)]
+    for c in order:
+        first.send_near(1, c, ahead[c])
     for s in range(2):
         @pl.when(jnp.logical_not(has[s]))
         def _(s=s):
@@ -371,8 +389,6 @@
         if v == 0:
             reduce_chip(2)
     wt[1, 0:head, :] = w15[...].astype(BF16)
-    for c in order:
-        first.send_far(1, c)
     for c in order[1:2]:
         first.forward(0, c)
     fi[p] = reduce_rest(2)
@@ -428,8 +444,11 @@
     def shaped(x):
         return x.reshape(x.shape[0] // (V * ch), V, ch, levels)
 
-    def near_copy(src, dst, ssem, rsem, h, s):
-        return remote(src.at[h, s], dst.at[h, 1 - s], ssem.at[h, s], rsem.at[h, 1 - s], m, near[s])
+    def edge_copy(h, s):
+        return remote(adjs.at[h, s], ahalo.at[h, 1 - s], ah_s.at[h], ah_r.at[h, 1 - s], m, near[s])
+
+    def hand_over(h, s):
+        return remote(ahalo.at[h, s], ahalo.at[h, s], ah_f.at[h], ah_r.at[h, s], mate, t)
 
     def single_copy(src, dst, ssem, rsem, s):
         return remote(src.at[s], dst.at[1 - s], ssem.at[s], rsem.at[1 - s], m, near[s])
@@ -444,9 +463,12 @@
             adjs15[0, 0:V] = thin[0:V]
             adjs15[1, 0:V] = thin[5 * V : 6 * V]
         for s in range(2):
+            @pl.when(has[s] & (p == s))
+            def _(s=s):
+                edge_copy(h, s).start()
+
             @pl.when(has[s])
             def _(s=s):
-                near_copy(adjs, ahalo, ah_s, ah_r, h, s).start()
                 if h:
                     single_copy(adjs15, ahalo15, a15_s, a15_r, s).start()
         for a in range(2):
@@ -456,9 +478,14 @@
 
     def adjoint_halo(h):
         for s in range(2):
-            @pl.when(has[s])
+            @pl.when(has[s] & (p == 1 - s))
             def _(s=s):
-                remote(ahalo.at[h, s], ahalo.at[h, s], ah_s.at[h, s], ah_r.at[h, s], m, near[s]).wait_recv()
+                hand_over(h, s).wait_recv()
+                hand_over(h, s).start()
+        for s in range(2):
+            @pl.when(has[s] & (p == s))
+            def _(s=s):
+                hand_over(h, s).wait_recv()
         adj[:, 0, half[h]] += ahalo[h, 0]
         adj[:, rows - 1, half[h]] += ahalo[h, 1]
 
@@ -473,18 +500,20 @@
                 gs[2 * h + outermost, s, k] = total
 
     def chain_open(h):
+        first.receive(h)
         for c in order:
-            first.receive(h, c)
             edge_increment(h, c)
         to_mate(h).start()
         reduce_chip(h)
         outer_send(h)
 
-    def chain_close(h):
+    def chain_close(h, between, after):
         full = stage_refs[h][3]
         full[p, :, 0:2] = reduce_rest(h)
+        between()
         outer_recv(h)
         back_to_mate(h).start()
+        after()
         back_from_mate(h).wait_recv()
 
     back_from_mate(2).wait_recv()
@@ -493,33 +522,48 @@
         first.forward(0, c)
     value = value + pick_inner(1)
 
+    def release(halo, h):
+        for c in order:
+            halo.send_far(h, c)
+
+    def between_a():
+        release(first, 1)
+        first.forward(1, order[0])
+
     chain_open(0)
     for c in order:
-        first.send_near(1, c)
-    chain_close(0)
-    for c in order[:2]:
+        first.send_near(1, c, jnp.logical_not(ahead[c]))
+    chain_close(0, between_a, lambda: None)
+    for c in order[1:2]:
         first.forward(1, c)
     value = value + pick_rim(0)
     weighted = jnp.where(live & early, wgt[...] * (value - innov[...]), 0.0)
     spread(weighted)
     adjoint_edges(0)
     fields(0, 0)
-    second.send(0)
+    for c in order:
+        second.send_turned(0, c)
+    for c in order:
+        second.send_near(0, c, ahead[c])
     for c in order[2:]:
         first.forward(1, c)
 
     chain_open(1)
+    for c in order:
+        second.send_near(0, c, jnp.logical_not(ahead[c]))
     adjoint_halo(0)
     fields(0, 1)
-    second.send(1)
-    for c in order:
+    second.send_close(1)
+    for c in order[:2]:
         second.forward(0, c)
-    chain_close(1)
+    chain_close(1, lambda: release(second, 0), lambda: release(second, 1))
+    for c in order[2:]:
+        second.forward(0, c)
     value = value + pick_rim(1)
     spread(jnp.where(live, wgt[...] * (value - innov[...]), 0.0))
     thin = adjoint_edges(1)
     fields(1, 0)
-    second.send(2)
+    second.send_close(2)
     for c in order:
         second.forward(1, c)
     for h in range(2):
@@ -527,8 +571,6 @@
         for a in range(rows - 4):
             adj[:, 2 + a, half[h]] = inner[a]
     adjoint_halo(1)
-    fields(1, 1)
-    second.send(3)
     for s in range(2):
         @pl.when(has[s])
         def _(s=s):
@@ -549,7 +591,14 @@
         @pl.when(has[s])
         def _(s=s):
             single_copy(gs15, gr15, g15_s, g15_r, s).start()
-    pair = 2 if members % 2 == 0 else 1
+    fields(1, 1)
+    for c in order:
+        second.send_far(2, c)
+    second.send_close(3)
+    for c in order:
+        second.send_far(3, c)
+
+    pair = group
 
     def inside(b, carry):
         ks = [b * pair + g for g in range(pair)]
@@ -576,36 +625,76 @@
     for c in order[2:]:
         second.forward(2, c)
     lax.fori_loop(stops[2], stops[3], inside, 0)
-    for c in order:
+
+    def outer_early(b, carry):
+        ks = [b * pair + g for g in range(pair)]
+        parts = []
+        for k in ks:
+            sides = []
+            for s in range(2):
+                for o in ((0, 1) if s == 0 else (1, 0)):
+                    at = lax.broadcasted_iota(jnp.int32, (ch, levels), 0)
+                    sides.append(jnp.where(at == ch - 1, 0.0, gr[o, s, k]))
+                    sides.append(gr[2, s, k] if o == 0 else jnp.zeros((ch, levels), F32))
+            parts.append(jnp.concatenate(sides, axis=0))
+        back = dot(em[...], jnp.concatenate(split2(jnp.concatenate(parts, axis=1)), axis=0))
+        hi, lo = split2(back)
+        for g, k in enumerate(ks):
+            part = slice(g * levels, (g + 1) * levels)
+            both = jnp.concatenate([hi[:, part], lo[:, part]], axis=1)
+            add = dot(both, lv_nn).reshape(4, cols, levels)
+            out[k, 0:2] += add[0:2]
+            out[k, rows - 2 : rows] += add[2:4]
+        return carry
+
+    for c in order[:1]:
         second.forward(3, c)
+    second.receive(0)
+    third = steps // 3
+    lax.fori_loop(0, third, outer_early, 0)
+    for c in order[1:2]:
+        second.forward(3, c)
+    lax.fori_loop(third, 2 * third, outer_early, 0)
+    for c in order[2:]:
+        second.forward(3, c)
+    lax.fori_loop(2 * third, steps, outer_early, 0)
+
+    i = lax.broadcasted_iota(jnp.int32, (4 * cols, 2 * ch + 16), 0)
+    j = lax.broadcasted_iota(jnp.int32, (4 * cols, 2 * ch + 16), 1)
+    q = lax.div(i, cols)
+    r = jnp.where(q < 2, q, q + rows - 4)
+    spot = j - 2 * ch
+    r2 = jnp.where(spot < 0, jnp.where(j < ch, -1, rows), jnp.where(spot < 2, spot - 2, spot - 2 + rows))
+    c2 = jnp.where(spot < 0, jnp.where(j < ch, j, j - ch) + ch, ch - 1)
+    last = band(r - r2) * (1.0 / 16.0) * column_weight(i - q * cols, c2, cols)
+    last = jnp.where(spot < 4, last, 0.0).astype(BF16)
+    last = jnp.concatenate([last, last], axis=1)
 
     for s in range(2):
         @pl.when(has[s])
         def _(s=s):
             remote(gr15.at[s], gr15.at[s], g15_s.at[s], g15_r.at[s], m, near[s]).wait_recv()
-    for g in range(3):
-        for c in order:
-            second.receive(g, c)
-
-    def outer(k):
-        sides = []
-        for s in range(2):
-            turn_rows = (0, 1) if s == 0 else (1, 0)
-            body = jnp.stack([jnp.concatenate([gr[o, s, k], gr[2 + o, s, k]], axis=0) for o in turn_rows])
-            at = lax.broadcasted_iota(jnp.int32, body.shape, 1)
-            line = jnp.stack([gr15[s, w, k : k + 1] for w in range(2)])
-            sides.append(jnp.where(at == ch - 1, jnp.broadcast_to(line, body.shape), body))
-        around = jnp.concatenate(sides, axis=0).reshape(4 * cols, levels)
-        back = dot(em[...], jnp.concatenate(split2(around), axis=0))
-        both = jnp.concatenate(split2(back), axis=1)
-        add = dot(both, lv_nn).reshape(4, cols, levels)
-        out[k, 0:2] += add[0:2]
-        out[k, rows - 2 : rows] += add[2:4]
-
-    for c in order:
-        second.receive(3, c)
-        for k in range(c * per, (c + 1) * per):
-            outer(k)
+    blank = jnp.zeros((12, levels), F32)
+
+    def outer_late(c):
+        ks = list(range(c * per, (c + 1) * per))
+        rowsets = []
+        for k in ks:
+            rowsets += [gr[3, 0, k], gr[3, 1, k]] + [gr15[s, w, k : k + 1] for s in range(2) for w in range(2)] + [blank]
+        both = jnp.concatenate(split2(jnp.concatenate(rowsets, axis=0)), axis=1)
+        hi, lo = split2(dot(both, lv_nn))
+        span = 2 * ch + 16
+        stack = jnp.concatenate(
+            [jnp.concatenate([x[g * span : (g + 1) * span] for g in range(len(ks))], axis=1) for x in (hi, lo)], axis=0)
+        add = dot(last, stack)
+        for g, k in enumerate(ks):
+            piece = add[:, g * levels : (g + 1) * levels].reshape(4, cols, levels)
+            out[k, 0:2] += piece[0:2]
+            out[k, rows - 2 : rows] += piece[2:4]
+
+    for c in order:
+        second.receive_chunk(3, c)
+        outer_late(c)
 
     first.drain()
     second.drain()
@@ -621,9 +710,13 @@
                 for d in range(n // 2):
                     outer_copy(h, s, d).wait_send()
 
-            @pl.when(has[s])
+            @pl.when(has[s] & (p == s))
             def _(h=h, s=s):
-                near_copy(adjs, ahalo, ah_s, ah_r, h, s).wait_send()
+                edge_copy(h, s).wait_send()
+
+            @pl.when(has[s] & (p == 1 - s))
+            def _(h=h, s=s):
+                hand_over(h, s).wait_send()
     for s in range(2):
         @pl.when(has[s])
         def _(s=s):
@@ -681,10 +774,10 @@
                 pltpu.VMEM((2, n // 2, V, ch, levels), F32), pltpu.VMEM((V, rows, cols, levels), F32), borders, borders,
                 small, small, slim, slim,
                 dma((9,)),
-                dma((2, 2, chunks)), dma((2, 2, chunks)), dma((2, chunks)), dma((2, chunks)),
-                dma((4, 2, chunks)), dma((4, 2, chunks)), dma((4, chunks)), dma((4, chunks)),
+                dma((2,)), dma((2, 2)), dma((1,)), dma((2, chunks)),
+                dma((2,)), dma((1, 2)), dma((2, chunks)), dma((1,)), dma((4, chunks)),
                 dma((3, n // 2 + 1)), dma((3, n // 2 + 1)),
-                dma((2, n // 2)), dma((2, n // 2)), dma((2, 2)), dma((2, 2)),
+                dma((2, n // 2)), dma((2, n // 2)), dma((2,)), dma((2, 2)), dma((2,)),
                 dma((2,)), dma((2,)), dma((2,)), dma((2,)),
             ],
             compiler_params=pltpu.CompilerParams(

time: 68.3 us -> 64.3 us (0.941)
  the two profiles are of different devices: /device:TPU:0 before, /device:TPU:16 now
where the time goes in v3:
time: 64.3 us; the launch traced here: 63.8 us
  Pallas kernels  61.7 us (96%)
  local copies, waits for them, and re-layouts  1.49 us (2%)
  between operations  0.66 us (1%)
    pallas_call x1, Pallas kernels, on_device(): pl.pallas_call(functools.partial(kernel, n, tiles, chunks), out_shape=jax...  61.7 us
    unnamed x1, local copies, waits for them, and re-layouts  1.49 us

profile of v3, /device:TPU:16, one launch (start us, length us, event | category | flops | bytes accessed | tf_op | source)
XLA Modules:
  0.0 63.8 jit_solution(8684636686389061224)
XLA Ops:
  0.7 61.7 %shard_map.82 = f32[20,8,32,128]{3,2,1,0:T(8,128)S(1)} custom-call(bf16[20,8,32,128]{3,2,1,0:T(8,128)(2,1)} %alpha_h.1, bf16[20,3,8,32,128]{4,3,2,1,0:T(8,128)(2,1)} %ens_h.1, bf16[128,128]{1,0:T(8,128)(2,1)} %loc_h.1, s32[1,2048]{1,0:T(1,128)} %col_h.1, s32[1,2048]{1,0:T(1,128)} %lev_h.1, s32[1]{0:T(128)S(6)} %copy.10.cnt, f32[1,2048]{1,0:T(1,128)} %innov_h.1, ...), custom_call_target="tpu_custom_call" | custom-call | tf_op jit(solution)/shard_map/pallas_call | solution.py:756
  62.4 1.5 %copy.11 = f32[20,8,32,128]{3,2,1,0:T(8,128)} copy(f32[20,8,32,128]{3,2,1,0:T(8,128)S(1)} %shard_map.82) | data formatting | bytes 5242880

commit v4 on v3

--- a/solution.py
+++ b/solution.py
@@ -544,13 +544,13 @@
     for c in order:
         second.send_turned(0, c)
     for c in order:
-        second.send_near(0, c, ahead[c])
+        second.send_near(0, c, (chunks - c) + n_out <= 4)
     for c in order[2:]:
         first.forward(1, c)
 
     chain_open(1)
     for c in order:
-        second.send_near(0, c, jnp.logical_not(ahead[c]))
+        second.send_near(0, c, jnp.logical_not((chunks - c) + n_out <= 4))
     adjoint_halo(0)
     fields(0, 1)
     second.send_close(1)

time: 64.3 us -> 63.6 us (0.989)
  Pallas kernels: 61.7 us -> 60.8 us
    pallas_call x1, Pallas kernels: 61.7 us -> 60.8 us  [on_device(): pl.pallas_call(functools.partial(kernel, n, tiles, chunks), out_shape=jax...]
where the time goes in v4:
time: 63.6 us; the launch traced here: 63 us
  Pallas kernels  60.8 us (96%)
  local copies, waits for them, and re-layouts  1.49 us (2%)
  between operations  0.66 us (1%)
    pallas_call x1, Pallas kernels, on_device(): pl.pallas_call(functools.partial(kernel, n, tiles, chunks), out_shape=jax...  60.8 us
    unnamed x1, local copies, waits for them, and re-layouts  1.49 us

profile of v4, /device:TPU:16, one launch (start us, length us, event | category | flops | bytes accessed | tf_op | source)
XLA Modules:
  0.0 63.0 jit_solution(4862690048092157469)
XLA Ops:
  0.7 60.8 %shard_map.82 = f32[20,8,32,128]{3,2,1,0:T(8,128)S(1)} custom-call(bf16[20,8,32,128]{3,2,1,0:T(8,128)(2,1)} %alpha_h.1, bf16[20,3,8,32,128]{4,3,2,1,0:T(8,128)(2,1)} %ens_h.1, bf16[128,128]{1,0:T(8,128)(2,1)} %loc_h.1, s32[1,2048]{1,0:T(1,128)} %col_h.1, s32[1,2048]{1,0:T(1,128)} %lev_h.1, s32[1]{0:T(128)S(6)} %copy.10.cnt, f32[1,2048]{1,0:T(1,128)} %innov_h.1, ...), custom_call_target="tpu_custom_call" | custom-call | tf_op jit(solution)/shard_map/pallas_call | solution.py:756
  61.5 1.5 %copy.11 = f32[20,8,32,128]{3,2,1,0:T(8,128)} copy(f32[20,8,32,128]{3,2,1,0:T(8,128)S(1)} %shard_map.82) | data formatting | bytes 5242880

commit v5 on v4

--- a/solution.py
+++ b/solution.py
@@ -39,7 +39,7 @@
 
 def kernel(n, tiles, chunks, alpha_h, ens_h, loc_h, col_h, lev_h, cnt, innov_h, wgt_h, out,
            av, ens, loc, col, lev, innov, wgt,
-           hs, hr, hl, gs, gr, gl, mm, sc, em, wt, w15, sent, e15,
+           hs, hr, hl, gs, gr, gl, mm, sc, em, el, wt, w15, sent, e15,
            bi, bi1, bi2, fi, b0, b01, b02, f0, b1, b11, b12, f1,
            iy, adj, adjs, ahalo, adjs15, ahalo15, gs15, gr15,
            in_sem, hs_s, hs_r, hl_s, hl_r, gs_s, gs_r, ge_r, gl_s, gl_r,
@@ -394,6 +394,18 @@
     fi[p] = reduce_rest(2)
     back_to_mate(2).start()
 
+    i = lax.broadcasted_iota(jnp.int32, (4 * cols, 2 * ch + 16), 0)
+    j = lax.broadcasted_iota(jnp.int32, (4 * cols, 2 * ch + 16), 1)
+    q = lax.div(i, cols)
+    r = jnp.where(q < 2, q, q + rows - 4)
+    spot = j - 2 * ch
+    r2 = jnp.where(spot < 0, jnp.where(j < ch, -1, rows), jnp.where(spot < 2, spot - 2, spot - 2 + rows))
+    c2 = jnp.where(spot < 0, jnp.where(j < ch, j, j - ch) + ch, ch - 1)
+    last = band(r - r2) * (1.0 / 16.0) * column_weight(i - q * cols, c2, cols)
+    last = jnp.where(spot < 4, last, 0.0).astype(BF16)
+    el[:, 0 : 2 * ch + 16] = last
+    el[:, 2 * ch + 16 :] = last
+
     e15[...] = jnp.zeros_like(e15)
     for s in range(2):
         for w in range(2):
@@ -541,16 +553,17 @@
     spread(weighted)
     adjoint_edges(0)
     fields(0, 0)
+    early_near = [(chunks - c) + n_out <= chunks for c in range(chunks)]
     for c in order:
         second.send_turned(0, c)
     for c in order:
-        second.send_near(0, c, (chunks - c) + n_out <= 4)
+        second.send_near(0, c, early_near[c])
     for c in order[2:]:
         first.forward(1, c)
 
     chain_open(1)
     for c in order:
-        second.send_near(0, c, jnp.logical_not((chunks - c) + n_out <= 4))
+        second.send_near(0, c, jnp.logical_not(early_near[c]))
     adjoint_halo(0)
     fields(0, 1)
     second.send_close(1)
@@ -659,17 +672,6 @@
         second.forward(3, c)
     lax.fori_loop(2 * third, steps, outer_early, 0)
 
-    i = lax.broadcasted_iota(jnp.int32, (4 * cols, 2 * ch + 16), 0)
-    j = lax.broadcasted_iota(jnp.int32, (4 * cols, 2 * ch + 16), 1)
-    q = lax.div(i, cols)
-    r = jnp.where(q < 2, q, q + rows - 4)
-    spot = j - 2 * ch
-    r2 = jnp.where(spot < 0, jnp.where(j < ch, -1, rows), jnp.where(spot < 2, spot - 2, spot - 2 + rows))
-    c2 = jnp.where(spot < 0, jnp.where(j < ch, j, j - ch) + ch, ch - 1)
-    last = band(r - r2) * (1.0 / 16.0) * column_weight(i - q * cols, c2, cols)
-    last = jnp.where(spot < 4, last, 0.0).astype(BF16)
-    last = jnp.concatenate([last, last], axis=1)
-
     for s in range(2):
         @pl.when(has[s])
         def _(s=s):
@@ -686,13 +688,14 @@
         span = 2 * ch + 16
         stack = jnp.concatenate(
             [jnp.concatenate([x[g * span : (g + 1) * span] for g in range(len(ks))], axis=1) for x in (hi, lo)], axis=0)
-        add = dot(last, stack)
+        add = dot(el[...], stack)
         for g, k in enumerate(ks):
             piece = add[:, g * levels : (g + 1) * levels].reshape(4, cols, levels)
             out[k, 0:2] += piece[0:2]
             out[k, rows - 2 : rows] += piece[2:4]
 
-    for c in order:
+    mixed = order[1:-1][::-1] + [0] + order[:1] if chunks > 1 else order
+    for c in mixed:
         second.receive_chunk(3, c)
         outer_late(c)
 
@@ -765,6 +768,7 @@
                 pltpu.VMEM((rows * cols, rows * cols), BF16),
                 pltpu.VMEM((4 * cols, 4 * cols), BF16),
                 pltpu.VMEM((4 * cols, 8 * cols), BF16),
+                pltpu.VMEM((4 * cols, 4 * ch + 32), BF16),
                 pltpu.VMEM((2, thin + V * (rows + 2) * ch, slots), BF16),
                 pltpu.VMEM((thin, slots), F32),
                 pltpu.VMEM((2 * levels, slots), BF16),

time: 63.6 us -> 63.2 us (level)
  no operation moved by 1% of the time
where the time goes in v5:
time: 63.2 us; the launch traced here: 63 us
  Pallas kernels  60.9 us (96%)
  local copies, waits for them, and re-layouts  1.49 us (2%)
  between operations  0.66 us (1%)
    pallas_call x1, Pallas kernels, on_device(): pl.pallas_call(functools.partial(kernel, n, tiles, chunks), out_shape=jax...  60.9 us
    unnamed x1, local copies, waits for them, and re-layouts  1.49 us

profile of v5, /device:TPU:16, one launch (start us, length us, event | category | flops | bytes accessed | tf_op | source)
XLA Modules:
  0.0 63.0 jit_solution(15671393560428740045)
XLA Ops:
  0.7 60.9 %shard_map.82 = f32[20,8,32,128]{3,2,1,0:T(8,128)S(1)} custom-call(bf16[20,8,32,128]{3,2,1,0:T(8,128)(2,1)} %alpha_h.1, bf16[20,3,8,32,128]{4,3,2,1,0:T(8,128)(2,1)} %ens_h.1, bf16[128,128]{1,0:T(8,128)(2,1)} %loc_h.1, s32[1,2048]{1,0:T(1,128)} %col_h.1, s32[1,2048]{1,0:T(1,128)} %lev_h.1, s32[1]{0:T(128)S(6)} %copy.10.cnt, f32[1,2048]{1,0:T(1,128)} %innov_h.1, ...), custom_call_target="tpu_custom_call" | custom-call | tf_op jit(solution)/shard_map/pallas_call | solution.py:759
  61.6 1.5 %copy.11 = f32[20,8,32,128]{3,2,1,0:T(8,128)} copy(f32[20,8,32,128]{3,2,1,0:T(8,128)S(1)} %shard_map.82) | data formatting | bytes 5242880

commit v6 on v5

--- a/solution.py
+++ b/solution.py
@@ -694,7 +694,7 @@
             out[k, 0:2] += piece[0:2]
             out[k, rows - 2 : rows] += piece[2:4]
 
-    mixed = order[1:-1][::-1] + [0] + order[:1] if chunks > 1 else order
+    mixed = order[1:-1][::-1] + order[:1] + [0] if chunks > 1 else order
     for c in mixed:
         second.receive_chunk(3, c)
         outer_late(c)

time: 63.2 us -> 63.2 us (level)
  no operation moved by 1% of the time
where the time goes in v6:
time: 63.2 us; the launch traced here: 63 us
  Pallas kernels  60.9 us (96%)
  local copies, waits for them, and re-layouts  1.49 us (2%)
  between operations  0.66 us (1%)
    pallas_call x1, Pallas kernels, on_device(): pl.pallas_call(functools.partial(kernel, n, tiles, chunks), out_shape=jax...  60.9 us
    unnamed x1, local copies, waits for them, and re-layouts  1.49 us

profile of v6, /device:TPU:16, one launch (start us, length us, event | category | flops | bytes accessed | tf_op | source)
XLA Modules:
  0.0 63.0 jit_solution(6280646843269933590)
XLA Ops:
  0.7 60.9 %shard_map.82 = f32[20,8,32,128]{3,2,1,0:T(8,128)S(1)} custom-call(bf16[20,8,32,128]{3,2,1,0:T(8,128)(2,1)} %alpha_h.1, bf16[20,3,8,32,128]{4,3,2,1,0:T(8,128)(2,1)} %ens_h.1, bf16[128,128]{1,0:T(8,128)(2,1)} %loc_h.1, s32[1,2048]{1,0:T(1,128)} %col_h.1, s32[1,2048]{1,0:T(1,128)} %lev_h.1, s32[1]{0:T(128)S(6)} %copy.10.cnt, f32[1,2048]{1,0:T(1,128)} %innov_h.1, ...), custom_call_target="tpu_custom_call" | custom-call | tf_op jit(solution)/shard_map/pallas_call | solution.py:759
  61.6 1.5 %copy.11 = f32[20,8,32,128]{3,2,1,0:T(8,128)} copy(f32[20,8,32,128]{3,2,1,0:T(8,128)S(1)} %shard_map.82) | data formatting | bytes 5242880
